TPU v7x, 512 devices: a whole 4x8x8 slice. The times are simulated.
512 devices in a mesh: text: 16 (over z, y_lo), det: 32 (over y_hi, x, core).
Axes of the slice: x: 4, y: 8 (y_hi: 4, y_lo: 2; y = y_hi * 2 + y_lo), z: 8, core: 2. Of those that a mesh axis runs over, the one named last changes fastest.
Arguments:
- prompt_embeds: bfloat16 [256, 16, 2048], P('text'), may hold values from -6 to 6
- prompt_len: int32 [256], P('text'), may hold values from 1 to 16
- norm_gain: float32 [2048], replicated, may hold values from 0.5 to 1.5
- w_up: bfloat16 [2048, 8192], P(None, 'det'), may hold values from -0.125 to 0.125
- w_down: bfloat16 [8192, 2048], P('det'), may hold values from -0.0625 to 0.0625
- final_gain: float32 [2048], replicated, may hold values from 0.25 to 1.75
- w_proj: bfloat16 [2048, 256], P('det'), may hold values from -0.125 to 0.125
- queries: bfloat16 [512, 1100, 256], P(('text', 'det')), may hold values from -6 to 6
- assign: int32 [512, 1100], P(('text', 'det')), may hold values from 0 to 511
- valid: int32 [512, 256], P(('text', 'det')), may hold values 0 or 1
Outputs:
- grad_up: float32 [2048, 8192], P('text', 'det')
- grad_down: float32 [8192, 2048], P('det', 'text')
- grad_proj: float32 [2048, 256], P('det')
- grad_queries: float32 [512, 1100, 256], P(('text', 'det'))
Inputs may be any that keep to these rules, and one draw needn't show every extreme that they name: `prompt_len`: every prompt uses at least its first token. `assign`: A value of 256 or more means the query has no concept.
All inputs are finite; a program needn't handle non-finite values. No bound on the sum of `valid` on one device may be relied on, other than what follows from the above.
Results may differ from a plain program's by a relative error of at most 0.025.
Values may be sent and summed in bfloat16 or wider, within the bound.
A program may use at most 64 MiB of HBM per device.

v0:
```python
import jax
import jax.numpy as jnp
from jax import lax
from jax.sharding import PartitionSpec as P

EPS = 1e-05
ALPHA = 0.25
LOGIT_BIAS = -2.0


def split_up(shard, dim, devices):
    before, after = (shard.shape[:dim], shard.shape[dim + 1 :])
    return jnp.moveaxis(shard.reshape(*before, devices, -1, *after), dim, 0)


def sum_at_owner(shard, axis, dim):
    tiles = split_up(shard, dim, lax.axis_size(axis))
    arrived = lax.all_to_all(tiles, axis, split_axis=0, concat_axis=0, tiled=True)
    return arrived.astype(jnp.float32).sum(axis=0)


def sent_to_all(shard, axis):
    copies = jnp.broadcast_to(shard, (lax.axis_size(axis), *shard.shape))
    return lax.all_to_all(copies, axis, split_axis=0, concat_axis=0, tiled=True)


def over_copies(shard, axis):
    return sent_to_all(shard, axis).sum(axis=0)


def together(arrays, axis):
    ends = [0]
    for a in arrays:
        ends.append(ends[-1] + a.size)
    subtotal = over_copies(jnp.concatenate([a.ravel() for a in arrays]), axis)
    return tuple((subtotal[b:e].reshape(a.shape) for a, b, e in zip(arrays, ends, ends[1:])))


def laid_out(tiles, dim):
    dims = list(tiles.shape[1:])
    dims[dim] *= tiles.shape[0]
    return jnp.moveaxis(tiles, 0, dim).reshape(dims)


def collect(shard, axis, dim):
    tiles = sent_to_all(shard, axis)
    return laid_out(tiles, dim)


def of_everyone(shard, axis):
    everything = sent_to_all(shard, axis)
    return jnp.sum(everything.astype(jnp.float32), axis=0)


def gelu_fn(values):
    return jax.nn.gelu(values, approximate=True)


def focal_total(scores, target, weight):
    log_pos = jax.nn.log_sigmoid(scores)
    log_neg = jax.nn.log_sigmoid(-scores)
    probab = jax.nn.sigmoid(scores)
    pos_term = -ALPHA * target * (1.0 - probab) ** 2 * log_pos
    neg_term = -(1.0 - ALPHA) * (1.0 - target) * probab**2 * log_neg
    return jnp.sum(weight * (pos_term + neg_term))


def body(
    prompt_embeds, prompt_len, norm_gain, w_up, w_down, final_gain, w_proj, queries, assign, valid
):
    per_group, prompt, model_width = prompt_embeds.shape
    tok_rows = per_group * prompt
    det_size = lax.axis_size("det")
    share = model_width // det_size
    offset = lax.axis_index("det") * share
    tokens = prompt_embeds.reshape(tok_rows, model_width).astype(jnp.float32)
    row_mean = jnp.mean(tokens, axis=1, keepdims=True)
    centred = tokens - row_mean
    variance = jnp.mean(centred * centred, axis=1, keepdims=True)
    normed = (centred * lax.rsqrt(variance + EPS) * norm_gain).astype(jnp.bfloat16)
    pre_act = jnp.dot(normed, w_up, preferred_element_type=jnp.float32)
    hidden_act, act_back = jax.vjp(gelu_fn, pre_act)
    hidden = hidden_act.astype(jnp.bfloat16)
    partial_out = jnp.dot(hidden, w_down, preferred_element_type=jnp.float32)
    position = lax.broadcasted_iota(jnp.int32, (per_group, prompt), 1)
    lengths = prompt_len.astype(jnp.float32)
    pool_weight = (position < prompt_len[:, None]).astype(jnp.float32) / lengths[:, None]
    own_part = sum_at_owner(partial_out.astype(jnp.bfloat16), "det", 1)
    layer_out = lax.dynamic_slice_in_dim(tokens, offset, share, 1) + own_part
    first_sum, second_sum = together(
        (jnp.sum(layer_out, axis=1), jnp.sum(layer_out * layer_out, axis=1)), "det"
    )
    out_mean = first_sum / model_width
    out_var = second_sum / model_width - out_mean * out_mean
    inv_scale = lax.rsqrt(out_var + EPS)[:, None]
    out_hat = (layer_out - out_mean[:, None]) * inv_scale
    gain_used = lax.dynamic_slice_in_dim(final_gain, offset, share, 0)
    final = out_hat * gain_used
    pooled_share = jnp.sum(
        final.reshape(per_group, prompt, share) * pool_weight[:, :, None], axis=1
    )
    pooled_low = pooled_share.astype(jnp.bfloat16)
    feat_part = jnp.dot(pooled_low, w_proj, preferred_element_type=jnp.float32)
    concept_feat = over_copies(feat_part, "det").astype(jnp.bfloat16)
    all_feat = collect(concept_feat, "text", 0)
    concept_count = all_feat.shape[0]
    img_count, query_count, query_width = queries.shape
    query_rows = img_count * query_count
    flat_queries = queries.reshape(query_rows, query_width)
    score_scale = query_width ** (-0.5)
    scores = (
        lax.dot_general(
            flat_queries, all_feat, (((1,), (1,)), ((), ())), preferred_element_type=jnp.float32
        )
        * score_scale
        + LOGIT_BIAS
    )
    column = lax.broadcasted_iota(jnp.int32, (img_count, query_count, concept_count), 2)
    target = (assign[:, :, None] == column).astype(jnp.float32).reshape(query_rows, concept_count)
    weight = jnp.broadcast_to(
        valid[:, None, :].astype(jnp.float32), (img_count, query_count, concept_count)
    ).reshape(query_rows, concept_count)
    score_grad = jax.grad(focal_total)(scores, target, weight).astype(jnp.bfloat16)
    query_grad = jnp.dot(score_grad, all_feat, preferred_element_type=jnp.float32) * score_scale
    images = img_count * lax.axis_size("text") * det_size
    feat_terms = lax.dot_general(
        score_grad, flat_queries, (((0,), (0,)), ((), ())), preferred_element_type=jnp.float32
    ) * (score_scale / images)
    feat_owned = sum_at_owner(feat_terms.astype(jnp.bfloat16), "text", 0)
    feat_grad = over_copies(feat_owned, "det")
    proj_part = jnp.dot(
        pooled_low.astype(jnp.float32).T, feat_grad, precision=lax.Precision.HIGHEST
    )
    proj_grad = of_everyone(proj_part.astype(jnp.bfloat16), "text").astype(jnp.float32)
    pooled_share_grad = jnp.dot(
        feat_grad, w_proj.astype(jnp.float32).T, precision=lax.Precision.HIGHEST
    )
    final_grad = (pooled_share_grad[:, None, :] * pool_weight[:, :, None]).reshape(tok_rows, share)
    hat_grad = final_grad * gain_used
    sum_first, sum_second = together(
        (jnp.sum(hat_grad, axis=1), jnp.sum(hat_grad * out_hat, axis=1)), "det"
    )
    share_grad = (
        (
            hat_grad
            - sum_first[:, None] / model_width
            - out_hat * (sum_second[:, None] / model_width)
        )
        * inv_scale
    ).astype(jnp.bfloat16)
    out_grad = lax.all_gather(share_grad, "det", axis=1, tiled=True)
    down_terms = lax.dot_general(
        hidden, out_grad, (((0,), (0,)), ((), ())), preferred_element_type=jnp.float32
    )
    down_grad = sum_at_owner(down_terms.astype(jnp.bfloat16), "text", 1)
    hidden_grad = lax.dot_general(
        out_grad, w_down, (((1,), (1,)), ((), ())), preferred_element_type=jnp.float32
    )
    pre_grad = act_back(hidden_grad)[0].astype(jnp.bfloat16)
    up_terms = lax.dot_general(
        normed, pre_grad, (((0,), (0,)), ((), ())), preferred_element_type=jnp.float32
    )
    up_grad = sum_at_owner(up_terms.astype(jnp.bfloat16), "text", 0)
    return (up_grad, down_grad, proj_grad, query_grad.reshape(img_count, query_count, query_width))


def solution(mesh):
    return jax.shard_map(
        body,
        mesh=mesh,
        in_specs=(
            P("text", None, None),
            P("text"),
            P(),
            P(None, "det"),
            P("det", None),
            P(),
            P("det", None),
            P(("text", "det"), None, None),
            P(("text", "det"), None),
            P(("text", "det"), None),
        ),
        out_specs=(
            P("text", "det"),
            P("det", "text"),
            P("det", None),
            P(("text", "det"), None, None),
        ),
        check_vma=False,
    )
```

profile of v0, /device:TPU:1, one launch (start us, length us, event | category | flops | bytes accessed | tf_op | source)
XLA Modules:
  0.0 295.7 jit_solution(17855576238334250466)
XLA Ops:
  7.2 1.6 convert_reduce_fusion.3
  9.8 1.7 fusion.58
  11.5 1.5 convolution_convert_fusion.2
  12.9 2.3 copy.35
  15.2 11.4 %all-to-all-start = ((bf16[32,256,64]{1,2,0:T(8,128)(2,1)}), bf16[32,256,64]{1,2,0:T(8,128)(2,1)}, u32[]{:S(2)}, u32[]{:S(2)}) async-start(bf16[32,256,64]{1,2,0:T(8,128)(2,1)} %bitcast.50), calls=%async_computation | async-start | bytes 2097152 | tf_op jit(solution)/shard_map/all_to_all | solution.py:18
  27.9 27.4 %all-to-all-done = bf16[32,256,64]{1,2,0:T(8,128)(2,1)} async-done(((bf16[32,256,64]{1,2,0:T(8,128)(2,1)}), bf16[32,256,64]{1,2,0:T(8,128)(2,1)}, u32[]{:S(2)}, u32[]{:S(2)}) %all-to-all-start) | async-done | bytes 1048608 | tf_op jit(solution)/shard_map/all_to_all | solution.py:18
  55.4 1.4 convert_reduce_fusion.2
  57.4 5.7 %all-to-all-start.1 = ((f32[32,1,512]{2,1,0:T(1,128)}), f32[32,1,512]{2,1,0:T(1,128)S(1)}, u32[]{:S(2)}, u32[]{:S(2)}) async-start(f32[32,1,512]{2,1,0:T(1,128)} %broadcast_in_dim.12), calls=%async_computation.1 | async-start | bytes 131072 | tf_op jit(solution)/shard_map/all_to_all | solution.py:24
  63.3 9.7 %all-to-all-done.1 = f32[32,1,512]{2,1,0:T(1,128)S(1)} async-done(((f32[32,1,512]{2,1,0:T(1,128)}), f32[32,1,512]{2,1,0:T(1,128)S(1)}, u32[]{:S(2)}, u32[]{:S(2)}) %all-to-all-start.1) | async-done | bytes 65568 | tf_op jit(solution)/shard_map/all_to_all | solution.py:24
  73.6 21.2 %all_to_all.52 = f32[32,16,256]{2,1,0:T(8,128)S(1)} all-to-all(f32[32,16,256]{2,1,0:T(8,128)S(1)} %broadcast_in_dim.13), channel_id=1, replica_groups=mesh['text'=16,'det'=32] {'det'}, dimensions={0} | all-to-all | bytes 1048576 | tf_op jit(solution)/shard_map/all_to_all | solution.py:24
  95.5 10.1 %all-to-all-start.3 = ((bf16[16,16,256]{2,1,0:T(8,128)(2,1)}), bf16[16,16,256]{2,1,0:T(8,128)(2,1)S(1)}, u32[]{:S(2)}, u32[]{:S(2)}) async-start(bf16[16,16,256]{2,1,0:T(8,128)(2,1)} %broadcast_in_dim.14), calls=%async_computation.3 | async-start | bytes 262144 | tf_op jit(solution)/shard_map/all_to_all | solution.py:24
  105.7 9.2 %all-to-all-done.3 = bf16[16,16,256]{2,1,0:T(8,128)(2,1)S(1)} async-done(((bf16[16,16,256]{2,1,0:T(8,128)(2,1)}), bf16[16,16,256]{2,1,0:T(8,128)(2,1)S(1)}, u32[]{:S(2)}, u32[]{:S(2)}) %all-to-all-start.3) | async-done | bytes 131104 | tf_op jit(solution)/shard_map/all_to_all | solution.py:24
  114.9 4.4 %fusion.11 = bf16[1100,256]{1,0:T(8,128)(2,1)S(1)} fusion(bf16[256,256]{1,0:T(8,128)(2,1)S(1)} %bitcast.52, bf16[1,1100,256]{2,1,0:T(8,128)(2,1)} %param.18, f32[256]{0:T(256)S(1)} %bitcast.56, s32[1100]{0:T(1024)S(1)} %reduce.5), kind=kOutput, calls=%fused_computation.33 | convolution fusion | flops 161356800 | bytes 1262896 | tf_op jit(solution)/shard_map/dot_general | solution.py:112
  119.4 0.8 copy-done.4
  120.6 10.7 %all_to_all.53 = bf16[16,16,256]{2,1,0:T(8,128)(2,1)S(1)} all-to-all(bf16[16,16,256]{2,1,0:T(8,128)(2,1)S(1)} %bitcast.55), channel_id=1, replica_groups=mesh['text'=16,'det'=32] {'text'}, dimensions={0} | all-to-all | bytes 262144 | tf_op jit(solution)/shard_map/all_to_all | solution.py:18
  131.3 0.9 broadcast_in_dim.15
  132.1 5.8 %all-to-all-start.5 = ((f32[32,16,256]{2,1,0:T(8,128)}), f32[32,16,256]{2,1,0:T(8,128)S(1)}, u32[]{:S(2)}, u32[]{:S(2)}) async-start(f32[32,16,256]{2,1,0:T(8,128)} %broadcast_in_dim.15), calls=%async_computation.5 | async-start | bytes 1048576 | tf_op jit(solution)/shard_map/all_to_all | solution.py:24
  138.1 17.0 %all-to-all-done.5 = f32[32,16,256]{2,1,0:T(8,128)S(1)} async-done(((f32[32,16,256]{2,1,0:T(8,128)}), f32[32,16,256]{2,1,0:T(8,128)S(1)}, u32[]{:S(2)}, u32[]{:S(2)}) %all-to-all-start.5) | async-done | bytes 524320 | tf_op jit(solution)/shard_map/all_to_all | solution.py:24
  155.8 15.2 %all_to_all.54 = f32[32,1,512]{2,1,0:T(1,128)S(1)} all-to-all(f32[32,1,512]{2,1,0:T(1,128)S(1)} %broadcast_in_dim.16), channel_id=1, replica_groups=mesh['text'=16,'det'=32] {'det'}, dimensions={0} | all-to-all | bytes 131072 | tf_op jit(solution)/shard_map/all_to_all | solution.py:24
  172.1 0.9 broadcast_in_dim.17
  172.9 3.6 %all-to-all-start.9 = ((bf16[16,64,256]{2,1,0:T(8,128)(2,1)}), bf16[16,64,256]{2,1,0:T(8,128)(2,1)S(1)}, u32[]{:S(2)}, u32[]{:S(2)}) async-start(bf16[16,64,256]{2,1,0:T(8,128)(2,1)} %broadcast_in_dim.17), calls=%async_computation.9 | async-start | bytes 1048576 | tf_op jit(solution)/shard_map/all_to_all | solution.py:24
  176.5 42.9 %all-gather.2.cloned.1.call-done = bf16[256,2048]{0,1:T(8,128)(2,1)} async-done(((bf16[256,64]{0,1:T(8,128)(2,1)}), bf16[256,2048]{0,1:T(8,128)(2,1)}) %all-gather.2.cloned.1.call-update) | async-done | bytes 1048592 | tf_op jit(solution)/shard_map/all_gather | solution.py:151
  219.4 3.6 %convolution_convert_fusion.1 = bf16[2048,256]{1,0:T(8,128)(2,1)} fusion(bf16[256,2048]{1,0:T(8,128)(2,1)S(1)} %multiply_convert_fusion, f32[256,256]{1,0:T(8,128)S(1)} %fusion.58, bf16[256,2048]{0,1:T(8,128)(2,1)} %all-gather.2.cloned.1.call-done, bf16[256,2048]{1,0:T(8,128)(2,1)S(1)} %copy-done), kind=kOutput, calls=%fused_computation.12 | convolution fusion | flops 538705920 | bytes 4456448 | tf_op jit(solution)/shard_map/dot_general | solution.py:160
  223.0 7.2 %all-to-all-start.7 = ((bf16[16,128,256]{2,1,0:T(8,128)(2,1)}), bf16[16,128,256]{2,1,0:T(8,128)(2,1)S(1)}, u32[]{:S(2)}, u32[]{:S(2)}) async-start(bf16[16,128,256]{2,1,0:T(8,128)(2,1)} %bitcast.51), calls=%async_computation.7 | async-start | bytes 2097152 | tf_op jit(solution)/shard_map/all_to_all | solution.py:18
  230.2 1.8 fusion.3
  232.0 1.3 copy.51
  233.2 22.9 %all-to-all-done.7 = bf16[16,128,256]{2,1,0:T(8,128)(2,1)S(1)} async-done(((bf16[16,128,256]{2,1,0:T(8,128)(2,1)}), bf16[16,128,256]{2,1,0:T(8,128)(2,1)S(1)}, u32[]{:S(2)}, u32[]{:S(2)}) %all-to-all-start.7) | async-done | bytes 1048608 | tf_op jit(solution)/shard_map/all_to_all | solution.py:18
  256.2 5.7 %all-to-all-start.8 = ((bf16[16,256,128]{2,1,0:T(8,128)(2,1)}), bf16[16,256,128]{2,1,0:T(8,128)(2,1)S(1)}, u32[]{:S(2)}, u32[]{:S(2)}) async-start(bf16[16,256,128]{2,1,0:T(8,128)(2,1)} %bitcast.49), calls=%async_computation.8 | async-start | bytes 2097152 | tf_op jit(solution)/shard_map/all_to_all | solution.py:18
  261.9 1.4 fusion.1
  263.3 5.7 %copy.41 = f32[1,1100,256]{2,0,1:T(1,128)} copy(f32[1,1100,256]{2,1,0:T(8,128)S(1)} %fusion.1) | data formatting | bytes 2252800
  270.5 17.5 %all-to-all-done.8 = bf16[16,256,128]{2,1,0:T(8,128)(2,1)S(1)} async-done(((bf16[16,256,128]{2,1,0:T(8,128)(2,1)}), bf16[16,256,128]{2,1,0:T(8,128)(2,1)S(1)}, u32[]{:S(2)}, u32[]{:S(2)}) %all-to-all-start.8) | async-done | bytes 1048608 | tf_op jit(solution)/shard_map/all_to_all | solution.py:18
  288.0 0.8 convert_reduce_fusion
  (68 shorter events, 8.1 us)
Async XLA Ops:
  7.2 4.3 %copy-start = (bf16[256,2048]{1,0:T(8,128)(2,1)S(1)}, bf16[256,2048]{1,0:T(8,128)(2,1)}, u32[]{:S(2)}) copy-start(bf16[256,2048]{1,0:T(8,128)(2,1)} %param.15) | copy-start | bytes 3145732
  7.2 1.6 copy-start.1
  7.2 2.2 copy-start.6
  15.2 11.4 %copy-start.9 = (s32[16]{0:T(128)S(1)}, s32[16]{0:T(128)}, u32[]{:S(2)}) copy-start(s32[16]{0:T(128)} %param.12) | copy-start | bytes 196
  15.2 40.1 %all-to-all-start = ((bf16[32,256,64]{1,2,0:T(8,128)(2,1)}), bf16[32,256,64]{1,2,0:T(8,128)(2,1)}, u32[]{:S(2)}, u32[]{:S(2)}) async-start(bf16[32,256,64]{1,2,0:T(8,128)(2,1)} %bitcast.50), calls=%async_computation | async-start | bytes 2097152 | tf_op jit(solution)/shard_map/all_to_all | solution.py:18
  27.1 46.3 %copy-start.5 = (bf16[64,256]{1,0:T(8,128)(2,1)S(1)}, bf16[64,256]{1,0:T(8,128)(2,1)}, u32[]{:S(2)}) copy-start(bf16[64,256]{1,0:T(8,128)(2,1)} %param.17) | copy-start | bytes 98308
  57.4 15.6 %all-to-all-start.1 = ((f32[32,1,512]{2,1,0:T(1,128)}), f32[32,1,512]{2,1,0:T(1,128)S(1)}, u32[]{:S(2)}, u32[]{:S(2)}) async-start(f32[32,1,512]{2,1,0:T(1,128)} %broadcast_in_dim.12), calls=%async_computation.1 | async-start | bytes 131072 | tf_op jit(solution)/shard_map/all_to_all | solution.py:24
  73.5 32.1 %copy-start.8 = (s32[1,256]{1,0:T(1,128)S(1)}, s32[1,256]{1,0:T(1,128)}, u32[]{:S(2)}) copy-start(s32[1,256]{1,0:T(1,128)} %param.20) | copy-start | bytes 3076
  73.5 32.1 %copy-start.7 = (s32[1,1100]{1,0:T(1,128)S(1)}, s32[1,1100]{1,0:T(1,128)}, u32[]{:S(2)}) copy-start(s32[1,1100]{1,0:T(1,128)} %param.19) | copy-start | bytes 13204
  95.5 19.4 %all-to-all-start.3 = ((bf16[16,16,256]{2,1,0:T(8,128)(2,1)}), bf16[16,16,256]{2,1,0:T(8,128)(2,1)S(1)}, u32[]{:S(2)}, u32[]{:S(2)}) async-start(bf16[16,16,256]{2,1,0:T(8,128)(2,1)} %broadcast_in_dim.14), calls=%async_computation.3 | async-start | bytes 262144 | tf_op jit(solution)/shard_map/all_to_all | solution.py:24
  114.9 5.3 %copy-start.10 = (bf16[1,1100,256]{2,1,0:T(8,128)(2,1)S(1)}, bf16[1,1100,256]{2,1,0:T(8,128)(2,1)}, u32[]{:S(2)}) copy-start(bf16[1,1100,256]{2,1,0:T(8,128)(2,1)} %param.18) | copy-start | bytes 1689604
  119.4 0.8 copy-start.4
  132.1 22.9 %all-to-all-start.5 = ((f32[32,16,256]{2,1,0:T(8,128)}), f32[32,16,256]{2,1,0:T(8,128)S(1)}, u32[]{:S(2)}, u32[]{:S(2)}) async-start(f32[32,16,256]{2,1,0:T(8,128)} %broadcast_in_dim.15), calls=%async_computation.5 | async-start | bytes 1048576 | tf_op jit(solution)/shard_map/all_to_all | solution.py:24
  138.0 81.4 %all-gather.2.cloned.1.call-start = ((), (), s32[]{:S(2)}) async-start(), calls=%async_computation.10 | async-start | bytes 1081344 | tf_op jit(solution)/shard_map/all_gather | solution.py:151
  172.9 50.1 %all-to-all-start.9 = ((bf16[16,64,256]{2,1,0:T(8,128)(2,1)}), bf16[16,64,256]{2,1,0:T(8,128)(2,1)S(1)}, u32[]{:S(2)}, u32[]{:S(2)}) async-start(bf16[16,64,256]{2,1,0:T(8,128)(2,1)} %broadcast_in_dim.17), calls=%async_computation.9 | async-start | bytes 1048576 | tf_op jit(solution)/shard_map/all_to_all | solution.py:24
  223.0 9.0 %copy-start.2 = (bf16[16,64,256]{2,1,0:T(8,128)(2,1)}, bf16[16,64,256]{2,1,0:T(8,128)(2,1)S(1)}, u32[]{:S(2)}) copy-start(bf16[16,64,256]{2,1,0:T(8,128)(2,1)S(1)} %all-to-all-done.9) | copy-start | bytes 1572868
  223.0 33.2 %all-to-all-start.7 = ((bf16[16,128,256]{2,1,0:T(8,128)(2,1)}), bf16[16,128,256]{2,1,0:T(8,128)(2,1)S(1)}, u32[]{:S(2)}, u32[]{:S(2)}) async-start(bf16[16,128,256]{2,1,0:T(8,128)(2,1)} %bitcast.51), calls=%async_computation.7 | async-start | bytes 2097152 | tf_op jit(solution)/shard_map/all_to_all | solution.py:18
  256.2 31.9 %all-to-all-start.8 = ((bf16[16,256,128]{2,1,0:T(8,128)(2,1)}), bf16[16,256,128]{2,1,0:T(8,128)(2,1)S(1)}, u32[]{:S(2)}, u32[]{:S(2)}) async-start(bf16[16,256,128]{2,1,0:T(8,128)(2,1)} %bitcast.49), calls=%async_computation.8 | async-start | bytes 2097152 | tf_op jit(solution)/shard_map/all_to_all | solution.py:18
  263.2 5.8 %copy-start.3 = (bf16[16,64,256]{2,1,0:T(8,128)(2,1)S(1)}, bf16[16,64,256]{2,1,0:T(8,128)(2,1)}, u32[]{:S(2)}) copy-start(bf16[16,64,256]{2,1,0:T(8,128)(2,1)} %copy-done.2) | copy-start | bytes 1572868
Sparse Core Ops, SparseCore 0:
  172.0 47.3 all-gather.1
where the time goes:
time: 298 us; the launch traced here: 296 us
  waiting for transfers between devices  147 us (49%)
  starting transfers between devices  49.6 us (17%)
  blocking collectives  47.1 us (16%)
  matrix products  15.2 us (5%)
  local copies, waits for them, and re-layouts  14.8 us (5%)
  between operations  14.4 us (5%)
  other arithmetic  8 us (3%)
    all_to_all x3, waiting for transfers between devices, sum_at_owner(): lax.all_to_all(tiles, axis, split_axis=0, concat_axis=0, tiled=True)  67.9 us
    all_gather x1, waiting for transfers between devices, body(): out_grad = lax.all_gather(share_grad, 'det', axis=1, tiled=True)  42.9 us
    all_to_all x2, blocking collectives, sent_to_all(): return lax.all_to_all(copies, axis, split_axis=0, concat_axis=0, tiled=True)  36.4 us
    all_to_all x4, waiting for transfers between devices, sent_to_all(): return lax.all_to_all(copies, axis, split_axis=0, concat_axis=0, tiled=True)  35.9 us
    all_to_all x4, starting transfers between devices, sent_to_all(): return lax.all_to_all(copies, axis, split_axis=0, concat_axis=0, tiled=True)  25.3 us
    all_to_all x3, starting transfers between devices, sum_at_owner(): lax.all_to_all(tiles, axis, split_axis=0, concat_axis=0, tiled=True)  24.3 us
    all_to_all x1, blocking collectives, sum_at_owner(): lax.all_to_all(tiles, axis, split_axis=0, concat_axis=0, tiled=True)  10.7 us
    unnamed x24, local copies, waits for them, and re-layouts  6.7 us
  transfers between devices with their start and end apart: 8, of which 7 were waited for; matrix products, arithmetic and copies ran while one was open for 6% of the time, Pallas kernels for 0%

commit v1 on v0

v1 whole, which is shorter than its diff:
```python
import jax
import jax.numpy as jnp
from jax import lax
from jax.experimental import pallas as pl
from jax.experimental.pallas import tpu as pltpu
from jax.sharding import PartitionSpec as P

EPS = 1e-05
ALPHA = 0.25
LOGIT_BIAS = -2.0
F32 = jnp.float32
BF16 = jnp.bfloat16
MESH = pl.DeviceIdType.MESH
GC = 0.7978845608028654
GA = 0.044715


class Place:
    def __init__(self):
        self.t = lax.axis_index("text")
        self.d = lax.axis_index("det")
        self.core = lax.rem(self.d, 2)
        self.chip = self.d // 2
        self.x = lax.rem(self.chip, 4)
        self.y = self.chip // 4
        self.z = self.t // 2
        self.yl = lax.rem(self.t, 2)

    def other_core(self):
        return {"det": self.d + 1 - 2 * self.core}

    def along_x(self, i):
        return {"det": (self.y * 4 + lax.rem(self.x + i, 4)) * 2 + self.core}

    def along_y(self, i):
        return {"det": (lax.rem(self.y + i, 4) * 4 + self.x) * 2 + self.core}

    def in_plane(self, i):
        return {"det": lax.rem(self.chip + i, 16) * 2 + self.core}

    def in_text(self, i):
        return {"text": lax.rem(self.t + i, 16)}

    def along_z(self, i):
        return {"text": lax.rem(self.z + i, 8) * 2 + self.yl}

    def across(self):
        return {"text": self.t + 1 - 2 * self.yl}

    def greet(self):
        barrier = pltpu.get_barrier_semaphore()
        pl.semaphore_signal(barrier, inc=1, device_id=self.other_core(), device_id_type=MESH)
        for i in range(1, 16):
            pl.semaphore_signal(barrier, inc=1, device_id=self.in_plane(i), device_id_type=MESH)
            pl.semaphore_signal(barrier, inc=1, device_id=self.in_text(i), device_id_type=MESH)

    def met(self):
        pl.semaphore_wait(pltpu.get_barrier_semaphore(), 31)


class Sends:
    def __init__(self, send_sems, recv_sems):
        self.send_sems, self.recv_sems, self.used = send_sems, recv_sems, 0
        self.flying = []

    def __call__(self, src, dst, to):
        copy = pltpu.make_async_remote_copy(
            src_ref=src,
            dst_ref=dst,
            send_sem=self.send_sems.at[self.used],
            recv_sem=self.recv_sems.at[self.used],
            device_id=to,
            device_id_type=MESH,
        )
        self.used += 1
        copy.start()
        self.flying.append(copy)
        return copy

    def drain(self):
        for copy in self.flying:
            copy.wait_send()


def at(i, n):
    return pl.ds(pl.multiple_of(i * n, n), n)


def dot(a, b, dims=((1,), (0,))):
    return lax.dot_general(a, b, (dims, ((), ())), preferred_element_type=F32)


def pool_weights(plen_ref, chip):
    length = jnp.full((16, 128), plen_ref[chip], jnp.int32)
    slot = lax.broadcasted_iota(jnp.int32, (16, 128), 0)
    weight = jnp.where(slot < length, 1.0 / length.astype(F32), 0.0)
    return weight[:, :1]


A_COPIES = 2 + 6 + 6 + 1 + 3 + 3 + 1 + 15 + 15 + 15


def forward_kernel(
    plen, tok, ngain, w_up, w_down, fgain, w_proj,
    feat_o, hid_o, nrm_o, gd_o, oh_o, inv_o, pool_o, wfull_o,
    cs, cr, xs, xr, ys, yr, lo, wfull, frow, psend, prow, allf, send_sems, recv_sems,
):
    me = Place()
    send = Sends(send_sems, recv_sems)
    core, chip, x, y, t = me.core, me.chip, me.x, me.y, me.t
    me.greet()
    tokens = tok[...].astype(F32)
    centred = tokens - jnp.mean(tokens, axis=1, keepdims=True)
    variance = jnp.mean(centred * centred, axis=1, keepdims=True)
    normed = (centred * lax.rsqrt(variance + EPS) * ngain[...]).astype(BF16)
    nrm_o[...] = normed
    pre = dot(normed, w_up[...])
    tanh = jnp.tanh(GC * (pre + GA * pre * pre * pre))
    hidden = (0.5 * pre * (1.0 + tanh)).astype(BF16)
    hid_o[...] = hidden
    gd_o[...] = 0.5 * (1.0 + tanh) + 0.5 * pre * (1.0 - tanh * tanh) * (GC * (1.0 + 3.0 * GA * pre * pre))
    wfull[y, x, core] = w_proj[...]
    for j in range(2):
        cs[j] = dot(hidden, w_down[:, at((1 - core) * 2 + j, 512)]).astype(BF16)
    me.met()
    to_core = [send(cs.at[j], cr.at[j], me.other_core()) for j in range(2)]
    w_y = [send(w_proj, wfull.at[y, x, core], me.along_y(i)) for i in (1, 2, 3)]
    to_x = []
    for j in range(2):
        own = dot(hidden, w_down[:, at(core * 2 + j, 512)])
        to_core[j].wait_recv()
        xs[j] = (own + cr[j].astype(F32)).astype(BF16).reshape(4, 4, 16, 512)
        to_x.append(
            [send(xs.at[j, :, lax.rem(x + i, 4)], xr.at[j, i - 1], me.along_x(i)) for i in (2, 1, 3)]
        )
    for copy in w_y:
        copy.wait_recv()
    to_y = []
    for j in range(2):
        for copy in to_x[j]:
            copy.wait_recv()
        total = xs[j, :, x].astype(F32)
        for i in range(3):
            total += xr[j, i].astype(F32)
        ys[j] = total.astype(BF16)
        to_y.append([send(ys.at[j, lax.rem(y + i, 4)], yr.at[j, i - 1], me.along_y(i)) for i in (2, 1, 3)])
    w_x = [send(wfull.at[:, x, core], wfull.at[:, x, core], me.along_x(i)) for i in (1, 2, 3)]
    for j in range(2):
        for copy in to_y[j]:
            copy.wait_recv()
        total = ys[j, y].astype(F32)
        for i in range(3):
            total += yr[j, i].astype(F32)
        lo[core, :, j * 512 : (j + 1) * 512] = total
    half = send(lo.at[core], lo.at[core], me.other_core())
    for copy in w_x:
        copy.wait_recv()
    w_core = send(wfull.at[:, :, core], wfull.at[:, :, core], me.other_core())
    half.wait_recv()
    layer_out = tok[at(chip, 16), :].astype(F32) + jnp.concatenate([lo[0], lo[1]], axis=1)
    centred = layer_out - jnp.mean(layer_out, axis=1, keepdims=True)
    inv_scale = lax.rsqrt(jnp.mean(centred * centred, axis=1, keepdims=True) + EPS)
    out_hat = centred * inv_scale
    oh_o[...] = out_hat
    inv_o[...] = jnp.broadcast_to(inv_scale, (16, 128))
    final = out_hat * fgain[...]
    pooled = jnp.sum(final * pool_weights(plen, chip), axis=0, keepdims=True)
    pooled_low = pooled.astype(BF16)
    w_core.wait_recv()
    feat = dot(jnp.broadcast_to(pooled_low, (16, 2048)), wfull[...].reshape(2048, 256))
    frow[chip] = feat[:1].astype(BF16).astype(F32)
    to_plane = [send(frow.at[chip], frow.at[chip], me.in_plane(i)) for i in range(1, 16)]
    rounded = pooled_low.astype(F32)
    for k in range(16):
        psend[k] = rounded[:, k * 128 : (k + 1) * 128]
    prow[chip] = psend[chip]
    pooled_to = [send(psend.at[lax.rem(chip + i, 16)], prow.at[chip], me.in_plane(i)) for i in range(1, 16)]
    wfull_o[...] = wfull[...].reshape(2048, 256)
    for copy in to_plane:
        copy.wait_recv()
    allf[t] = jnp.concatenate([frow[k] for k in range(16)], axis=0).astype(BF16)
    to_text = [send(allf.at[t], allf.at[t], me.in_text(i)) for i in range(1, 16)]
    for copy in pooled_to:
        copy.wait_recv()
    pool_o[...] = jnp.concatenate([prow[k] for k in range(16)], axis=0).astype(BF16)
    for copy in to_text:
        copy.wait_recv()
    feat_o[...] = allf[...].reshape(256, 256)
    send.drain()


B_COPIES = 1 + 15 + 15 + 1 + 15 + 3 + 12 + 15 + 2 * 15


def backward_kernel(
    plen, ft, hid, nrm, gd, oh, inv, pool, wfull, w_down, fgain,
    up_o, down_o, proj_o,
    cs, cr, ts, tr, ps, pr, fgb, fgs, pj, pjf, og, h_t, n_t, ds, dyr, dz, dr, us, uyr, uz, ur,
    send_sems, recv_sems,
):
    me = Place()
    send = Sends(send_sems, recv_sems)
    core, chip, x, y, t, z, yl = me.core, me.chip, me.x, me.y, me.t, me.z, me.yl
    me.greet()
    cs[...] = ft[:, at(1 - core, 128)].astype(BF16)
    me.met()
    to_core = send(cs, cr, me.other_core())
    h_t[...] = hid[...].T
    to_core.wait_recv()
    ts[...] = (ft[:, at(core, 128)] + cr[...].astype(F32)).astype(BF16).reshape(16, 16, 128)
    to_text = [send(ts.at[lax.rem(t + i, 16)], tr.at[i - 1], me.in_text(i)) for i in range(1, 16)]
    n_t[...] = nrm[...].T
    total = ts[t].astype(F32)
    for i in range(15):
        to_text[i].wait_recv()
        total += tr[i].astype(F32)
    ps[...] = total
    to_plane = [send(ps, pr.at[i - 1], me.in_plane(i)) for i in range(1, 16)]
    for i in range(15):
        to_plane[i].wait_recv()
        total += pr[i]
    fgb[core] = total
    half = send(fgb.at[core], fgb.at[core], me.other_core())
    half.wait_recv()
    feat_grad = jnp.concatenate([fgb[0], fgb[1]], axis=1)
    fgs[...] = feat_grad
    row = fgs[pl.ds(chip, 1), :]
    high = row.astype(BF16).astype(F32)
    middle = (row - high).astype(BF16).astype(F32)
    low = row - high - middle
    part = lax.broadcasted_iota(jnp.int32, (16, 256), 0)
    rows = jnp.where(part == 0, high, jnp.where(part == 1, middle, jnp.where(part == 2, low, 0.0)))
    pooled_grad = jnp.sum(dot(rows.astype(BF16), wfull[...], ((1,), (1,))), axis=0, keepdims=True)
    hat = pooled_grad * fgain[...]
    out_hat = oh[...]
    first = jnp.mean(hat, axis=1, keepdims=True)
    second = jnp.mean(hat * out_hat, axis=1, keepdims=True)
    scale = pool_weights(plen, chip) * inv[:, :1]
    out_grad = ((hat - first - out_hat * second) * scale).astype(BF16)
    og[0, y, x] = out_grad[:, :1024]
    og[1, y, x] = out_grad[:, 1024:]
    mine = og.at[core, y, x]
    to_y = [send(mine, mine, me.along_y(i)) for i in (2, 1, 3)]
    waves = [[send(mine, mine, me.along_x(i)) for i in (2, 1, 3)]]
    pj[t, :, :256] = feat_grad.astype(BF16)
    pj[t, :, 256:] = pool[...]
    to_other = []
    pj_to = [send(pj.at[t], pj.at[t], me.in_text(i)) for i in range(1, 16)]
    for copy, i in ((to_y[1], 1), (to_y[2], 3), (to_y[0], 2)):
        copy.wait_recv()
        block = og.at[core, lax.rem(y + 4 - i, 4), x]
        waves.append([send(block, block, me.along_x(j)) for j in (2, 1, 3)])
        to_other.append(send(block, block, me.other_core()))
    for wave, i in zip(waves, (0, 1, 3, 2)):
        for copy, j in zip(wave, (2, 1, 3)):
            copy.wait_recv()
            block = og.at[core, lax.rem(y + 4 - i, 4), lax.rem(x + 4 - j, 4)]
            to_other.append(send(block, block, me.other_core()))
    for copy in to_other:
        copy.wait_recv()
    order = (4, 3, 5, 2, 6, 1, 7, 0)

    def exchange(parts, arrived):
        copies = {}
        for i in order:
            spot = lax.rem(z + i, 8)
            copies[i] = send(parts.at[spot, 1 - yl], arrived.at[i], me.across())
        return copies

    def onward(copies, parts, arrived, staged, landed):
        copies_z = {}
        for i in order[:-1]:
            copies[i].wait_recv()
            staged[i - 1] = (parts[lax.rem(z + i, 8), yl].astype(F32) + arrived[i].astype(F32)).astype(BF16)
            copies_z[i] = send(staged.at[i - 1], landed.at[i - 1], me.along_z(i))
        return copies_z

    def finish(copies, copies_z, parts, arrived, landed, out):
        copies[0].wait_recv()
        total = parts[z, yl].astype(F32) + arrived[0].astype(F32)
        for i in (1, 7, 2, 6, 3, 5, 4):
            copies_z[i].wait_recv()
            total += landed[i - 1].astype(F32)
        out[...] = total

    halves = [og[h].reshape(256, 1024) for h in range(2)]
    for h in range(2):
        product = dot(h_t[...], halves[h]).astype(BF16)
        for k in range(8):
            ds[h * 4 + k // 2, k % 2] = product[:, k * 128 : (k + 1) * 128]
    down_y = exchange(ds, dyr)
    hidden_grad = dot(halves[0], w_down[:, :1024], ((1,), (1,))) + dot(halves[1], w_down[:, 1024:], ((1,), (1,)))
    pre_grad = (hidden_grad * gd[...]).astype(BF16)
    us[...] = dot(n_t[...], pre_grad).astype(BF16).reshape(8, 2, 128, 256)
    up_y = exchange(us, uyr)
    down_z = onward(down_y, ds, dyr, dz, dr)
    up_z = onward(up_y, us, uyr, uz, ur)
    for copy in pj_to:
        copy.wait_recv()
    pjf[...] = dot(pj[:, :, 256:].reshape(256, 128), pj[:, :, :256].reshape(256, 256), ((0,), (0,)))
    proj_o[...] = pjf[at(core, 64), :]
    finish(down_y, down_z, ds, dyr, dr, down_o)
    finish(up_y, up_z, us, uyr, ur, up_o)
    send.drain()


def vmem(n):
    return [pl.BlockSpec(memory_space=pltpu.VMEM)] * n


def forward(plen, tok, ngain, w_up, w_down, fgain, w_proj):
    return pl.pallas_call(
        forward_kernel,
        name="forward",
        in_specs=[pl.BlockSpec(memory_space=pltpu.SMEM)] + vmem(6),
        out_specs=vmem(8),
        out_shape=(
            jax.ShapeDtypeStruct((256, 256), BF16),
            jax.ShapeDtypeStruct((256, 256), BF16),
            jax.ShapeDtypeStruct((256, 2048), BF16),
            jax.ShapeDtypeStruct((256, 256), F32),
            jax.ShapeDtypeStruct((16, 2048), F32),
            jax.ShapeDtypeStruct((16, 128), F32),
            jax.ShapeDtypeStruct((16, 128), BF16),
            jax.ShapeDtypeStruct((2048, 256), BF16),
        ),
        scratch_shapes=[
            pltpu.VMEM((2, 256, 512), BF16),
            pltpu.VMEM((2, 256, 512), BF16),
            pltpu.VMEM((2, 4, 4, 16, 512), BF16),
            pltpu.VMEM((2, 3, 4, 16, 512), BF16),
            pltpu.VMEM((2, 4, 16, 512), BF16),
            pltpu.VMEM((2, 3, 16, 512), BF16),
            pltpu.VMEM((2, 16, 1024), F32),
            pltpu.VMEM((4, 4, 2, 64, 256), BF16),
            pltpu.VMEM((16, 1, 256), F32),
            pltpu.VMEM((16, 1, 128), F32),
            pltpu.VMEM((16, 1, 128), F32),
            pltpu.VMEM((16, 16, 256), BF16),
            pltpu.SemaphoreType.DMA((A_COPIES,)),
            pltpu.SemaphoreType.DMA((A_COPIES,)),
        ],
        compiler_params=pltpu.CompilerParams(
            collective_id=0, has_side_effects=True, vmem_limit_bytes=40 << 20
        ),
    )(plen, tok, ngain, w_up, w_down, fgain, w_proj)


def backward(plen, ft, hid, nrm, gd, oh, inv, pool, wfull, w_down, fgain):
    return pl.pallas_call(
        backward_kernel,
        name="backward",
        in_specs=[pl.BlockSpec(memory_space=pltpu.SMEM)] + vmem(10),
        out_specs=vmem(3),
        out_shape=(
            jax.ShapeDtypeStruct((128, 256), F32),
            jax.ShapeDtypeStruct((256, 128), F32),
            jax.ShapeDtypeStruct((64, 256), F32),
        ),
        scratch_shapes=[
            pltpu.VMEM((256, 128), BF16),
            pltpu.VMEM((256, 128), BF16),
            pltpu.VMEM((16, 16, 128), BF16),
            pltpu.VMEM((15, 16, 128), BF16),
            pltpu.VMEM((16, 128), F32),
            pltpu.VMEM((15, 16, 128), F32),
            pltpu.VMEM((2, 16, 128), F32),
            pltpu.VMEM((16, 256), F32),
            pltpu.VMEM((16, 16, 384), BF16),
            pltpu.VMEM((128, 256), F32),
            pltpu.VMEM((2, 4, 4, 16, 1024), BF16),
            pltpu.VMEM((256, 256), BF16),
            pltpu.VMEM((2048, 256), BF16),
            pltpu.VMEM((8, 2, 256, 128), BF16),
            pltpu.VMEM((8, 256, 128), BF16),
            pltpu.VMEM((7, 256, 128), BF16),
            pltpu.VMEM((7, 256, 128), BF16),
            pltpu.VMEM((8, 2, 128, 256), BF16),
            pltpu.VMEM((8, 128, 256), BF16),
            pltpu.VMEM((7, 128, 256), BF16),
            pltpu.VMEM((7, 128, 256), BF16),
            pltpu.SemaphoreType.DMA((B_COPIES,)),
            pltpu.SemaphoreType.DMA((B_COPIES,)),
        ],
        compiler_params=pltpu.CompilerParams(
            collective_id=1, has_side_effects=True, vmem_limit_bytes=40 << 20
        ),
    )(plen, ft, hid, nrm, gd, oh, inv, pool, wfull, w_down, fgain)


def focal_total(scores, target, weight):
    log_pos = jax.nn.log_sigmoid(scores)
    log_neg = jax.nn.log_sigmoid(-scores)
    probab = jax.nn.sigmoid(scores)
    pos_term = -ALPHA * target * (1.0 - probab) ** 2 * log_pos
    neg_term = -(1.0 - ALPHA) * (1.0 - target) * probab**2 * log_neg
    return jnp.sum(weight * (pos_term + neg_term))


def body(
    prompt_embeds, prompt_len, norm_gain, w_up, w_down, final_gain, w_proj, queries, assign, valid
):
    tok = prompt_embeds.reshape(256, 2048)
    ngain, fgain = norm_gain.reshape(1, 2048), final_gain.reshape(1, 2048)
    all_feat, hid, nrm, gd, oh, inv, pool, wfull = forward(
        prompt_len, tok, ngain, w_up, w_down, fgain, w_proj
    )
    img_count, query_count, query_width = queries.shape
    query_rows = img_count * query_count
    concept_count = all_feat.shape[0]
    flat_queries = queries.reshape(query_rows, query_width)
    score_scale = query_width ** (-0.5)
    scores = dot(flat_queries, all_feat, ((1,), (1,))) * score_scale + LOGIT_BIAS
    column = lax.broadcasted_iota(jnp.int32, (img_count, query_count, concept_count), 2)
    target = (assign[:, :, None] == column).astype(F32).reshape(query_rows, concept_count)
    weight = jnp.broadcast_to(
        valid[:, None, :].astype(F32), (img_count, query_count, concept_count)
    ).reshape(query_rows, concept_count)
    score_grad = jax.grad(focal_total)(scores, target, weight).astype(BF16)
    query_grad = dot(score_grad, all_feat) * score_scale
    images = img_count * lax.axis_size("text") * lax.axis_size("det")
    feat_terms = dot(score_grad, flat_queries, ((0,), (0,))) * (score_scale / images)
    up_grad, down_grad, proj_grad = backward(
        prompt_len, feat_terms, hid, nrm, gd, oh, inv, pool, wfull, w_down, fgain
    )
    return (up_grad, down_grad, proj_grad, query_grad.reshape(img_count, query_count, query_width))


def solution(mesh):
    return jax.shard_map(
        body,
        mesh=mesh,
        in_specs=(
            P("text", None, None),
            P("text"),
            P(),
            P(None, "det"),
            P("det", None),
            P(),
            P("det", None),
            P(("text", "det"), None, None),
            P(("text", "det"), None),
            P(("text", "det"), None),
        ),
        out_specs=(
            P("text", "det"),
            P("det", "text"),
            P("det", None),
            P(("text", "det"), None, None),
        ),
        check_vma=False,
    )
```

time: 298 us -> 136 us (0.46)
  waiting for transfers between devices: 147 us -> 0 us
  Pallas kernels: 0 us -> 113 us
  starting transfers between devices: 49.6 us -> 0 us
  blocking collectives: 47.1 us -> 0 us
  between operations: 14.4 us -> 0.71 us
  matrix products: 15.2 us -> 4.43 us
  other arithmetic: 8 us -> 1.45 us
    pallas_call x0 -> x2, Pallas kernels: none -> 113 us  [the longest x1 65.9 us: backward(): pl.pallas_call(backward_kernel, name='backward', in_specs=[pl.BlockSpec(m...]
    all_to_all x7 -> x0, waiting for transfers between devices: 104 us -> none  [the longest x3 67.9 us: sum_at_owner(): lax.all_to_all(tiles, axis, split_axis=0, concat_axis=0, tiled=True)]
    all_to_all x7 -> x0, starting transfers between devices: 49.5 us -> none  [the longest x4 25.3 us: sent_to_all(): return lax.all_to_all(copies, axis, split_axis=0, concat_axis=0, tiled=True)]
    all_to_all x3 -> x0, blocking collectives: 47.1 us -> none  [the longest x2 36.4 us: sent_to_all(): return lax.all_to_all(copies, axis, split_axis=0, concat_axis=0, tiled=True)]
    all_gather x1 -> x0, waiting for transfers between devices: 42.9 us -> none  [body(): out_grad = lax.all_gather(share_grad, 'det', axis=1, tiled=True)]
    dot_general x10 -> x3, matrix products: 15.2 us -> 4.43 us  [dot(): return lax.dot_general(a, b, (dims, ((), ())), preferred_element_type=F32)]
    unnamed x24 -> x22, local copies, waits for them, and re-layouts: 6.7 us -> 15 us
    reduce_sum x15 -> x0, other arithmetic: 6.36 us -> none  [the longest x4 3 us: sum_at_owner(): return arrived.astype(jnp.float32).sum(axis=0)]
  transfers between devices with their start and end apart: 8 -> 0, of which waited for: 7 -> 0; matrix products, arithmetic and copies ran while one was open for 6% -> 0% of each run, Pallas kernels for 0% -> 0%
where the time goes in v1:
time: 136 us; the launch traced here: 135 us
  Pallas kernels  113 us (83%)
  local copies, waits for them, and re-layouts  15 us (11%)
  matrix products  4.43 us (3%)
  other arithmetic  1.45 us (1%)
    pallas_call x1, Pallas kernels, backward(): pl.pallas_call(backward_kernel, name='backward', in_specs=[pl.BlockSpec(m...  65.9 us
    pallas_call x1, Pallas kernels, forward(): pl.pallas_call(forward_kernel, name='forward', in_specs=[pl.BlockSpec(mem...  47.5 us
    unnamed x22, local copies, waits for them, and re-layouts  15 us
    dot_general x3, matrix products, dot(): return lax.dot_general(a, b, (dims, ((), ())), preferred_element_type=F32)  4.43 us

profile of v1, /device:TPU:1, one launch (start us, length us, event | category | flops | bytes accessed | tf_op | source)
XLA Modules:
  0.0 135.1 jit_solution(13573962423317708258)
XLA Ops:
  0.6 0.0 copy-start
  0.6 0.7 convert_element_type.21
  1.4 0.7 reduce
  2.1 0.0 copy-start.1
  2.1 1.2 copy-done.1
  3.3 0.0 copy-start.3
  3.3 1.2 copy-done.3
  4.5 0.0 copy-start.4
  4.6 1.2 copy-done.4
  5.8 0.0 copy-start.5
  5.8 0.8 copy-done.5
  6.5 0.0 copy-start.6
  6.5 0.7 copy-done.6
  7.2 0.0 copy-start.7
  7.2 0.7 copy-done.7
  7.9 0.0 copy-start.8
  7.9 0.7 copy-done.8
  8.6 47.5 %forward.1 = (bf16[256,256]{1,0:T(8,128)(2,1)S(1)}, bf16[256,256]{1,0:T(8,128)(2,1)S(1)}, bf16[256,2048]{1,0:T(8,128)(2,1)S(1)}, f32[256,256]{1,0:T(8,128)S(1)},...) custom-call(s32[16]{0:T(128)S(1)} %copy-done.8, ...), custom_call_target="tpu_custom_call" | custom-call | tf_op jit(solution)/shard_map/forward/pallas_call | solution.py:312
  56.1 0.0 copy-done
  56.1 3.8 %fusion.9 = bf16[1100,256]{1,0:T(8,128)(2,1)S(1)} fusion(bf16[256,256]{1,0:T(8,128)(2,1)S(1)} %get-tuple-element.19, bf16[1,1100,256]{2,1,0:T(8,128)(2,1)S(1)} %copy-done, f32[256]{0:T(256)S(1)} %bitcast.23, s32[1100]{0:T(1024)S(1)} %reduce), kind=kOutput, calls=%fused_computation.23 | convolution fusion | flops 161356800 | bytes 1262896 | tf_op jit(solution)/shard_map/dot_general | solution.py:90
  59.9 0.0 copy-start.2
  59.9 0.4 convolution_multiply_fusion.2.ft
  60.3 0.8 copy-done.2
  61.1 65.9 %backward.1 = (f32[128,256]{1,0:T(8,128)S(1)}, f32[256,128]{1,0:T(8,128)S(1)}, f32[64,256]{1,0:T(8,128)S(1)}) custom-call(s32[16]{0:T(128)S(1)} %copy-done.8, f32[256,256]{1,0:T(8,128)S(1)} %convolution_multiply_fusion.2.ft, bf16[256,256]{1,0:T(8,128)(2,1)S(1)} %get-tuple-element.24.hid, bf16[256,2048]{1,0:T(8,128)(2,1)S(1)} %get-tuple-element.25.nrm, ...), custom_call_target="tpu_custom_call" | custom-call | tf_op jit(solution)/shard_map/backward/pallas_call | solution.py:350
  127.1 0.3 fusion.1
  127.4 5.7 %copy.14 = f32[1,1100,256]{2,0,1:T(1,128)} copy(f32[1,1100,256]{2,1,0:T(8,128)S(1)} %fusion.1) | data formatting | bytes 2252800
  133.1 0.7 copy.18
  133.8 0.7 copy.19
  134.4 0.6 copy.20
Async XLA Ops:
  0.6 55.5 %copy-start = (bf16[1,1100,256]{2,1,0:T(8,128)(2,1)S(1)}, bf16[1,1100,256]{2,1,0:T(8,128)(2,1)}, u32[]{:S(2)}) copy-start(bf16[1,1100,256]{2,1,0:T(8,128)(2,1)} %param.18) | copy-start | bytes 1689604
  2.1 1.2 copy-start.1
  3.3 1.2 copy-start.3
  4.5 1.2 copy-start.4
  5.8 0.8 copy-start.5
  6.5 0.7 copy-start.6
  7.2 0.7 copy-start.7
  7.9 0.7 copy-start.8
  59.9 1.2 copy-start.2

commit v2 on v1

v2 whole, which is shorter than its diff:
```python
import jax
import jax.numpy as jnp
from jax import lax
from jax.experimental import pallas as pl
from jax.experimental.pallas import tpu as pltpu
from jax.sharding import PartitionSpec as P

EPS = 1e-05
ALPHA = 0.25
LOGIT_BIAS = -2.0
F32 = jnp.float32
BF16 = jnp.bfloat16
MESH = pl.DeviceIdType.MESH
GC = 0.7978845608028654
GA = 0.044715


class Place:
    def __init__(self):
        self.t = lax.axis_index("text")
        self.d = lax.axis_index("det")
        self.core = lax.rem(self.d, 2)
        self.chip = self.d // 2
        self.x = lax.rem(self.chip, 4)
        self.y = self.chip // 4
        self.z = self.t // 2
        self.yl = lax.rem(self.t, 2)

    def other_core(self):
        return {"det": self.d + 1 - 2 * self.core}

    def along_x(self, i):
        return {"det": (self.y * 4 + lax.rem(self.x + i, 4)) * 2 + self.core}

    def along_y(self, i):
        return {"det": (lax.rem(self.y + i, 4) * 4 + self.x) * 2 + self.core}

    def in_plane(self, i, swap=0):
        core = 1 - self.core if swap else self.core
        return {"det": lax.rem(self.chip + i, 16) * 2 + core}

    def in_text(self, i):
        return {"text": lax.rem(self.t + i, 16)}

    def along_z(self, i):
        return {"text": lax.rem(self.z + i, 8) * 2 + self.yl}

    def across(self):
        return {"text": self.t + 1 - 2 * self.yl}

    def greet(self):
        barrier = pltpu.get_barrier_semaphore()
        pl.semaphore_signal(barrier, inc=1, device_id=self.other_core(), device_id_type=MESH)
        for i in range(1, 16):
            pl.semaphore_signal(barrier, inc=1, device_id=self.in_plane(i), device_id_type=MESH)
            pl.semaphore_signal(barrier, inc=1, device_id=self.in_plane(i, 1), device_id_type=MESH)
            pl.semaphore_signal(barrier, inc=1, device_id=self.in_text(i), device_id_type=MESH)

    def met(self):
        pl.semaphore_wait(pltpu.get_barrier_semaphore(), 46)


class Sends:
    def __init__(self, send_sems, recv_sems):
        self.send_sems, self.recv_sems, self.used = send_sems, recv_sems, 0
        self.flying = []

    def __call__(self, src, dst, to):
        copy = pltpu.make_async_remote_copy(
            src_ref=src,
            dst_ref=dst,
            send_sem=self.send_sems.at[self.used],
            recv_sem=self.recv_sems.at[self.used],
            device_id=to,
            device_id_type=MESH,
        )
        self.used += 1
        copy.start()
        self.flying.append(copy)
        return copy

    def drain(self):
        for copy in self.flying:
            copy.wait_send()


def at(i, n):
    return pl.ds(pl.multiple_of(i * n, n), n)


def dot(a, b, dims=((1,), (0,))):
    return lax.dot_general(a, b, (dims, ((), ())), preferred_element_type=F32)


def pool_weights(plen, chip):
    lane = lax.broadcasted_iota(jnp.int32, (16, 16), 1)
    length = jnp.sum(jnp.where(lane == chip, plen[...], 0).astype(F32), axis=1, keepdims=True)
    slot = lax.broadcasted_iota(jnp.int32, (16, 1), 0).astype(F32)
    return jnp.where(slot < length, 1.0 / length, 0.0)


COPIES = 2 + 3 + 6 + 6 + 3 + 1 + 1 + 15 + 15 + 15 + 1 + 15 + 31 + 15 + 15 + 3 + 12 + 15 + 30
SCORE_SCALE = 256 ** (-0.5)
IMAGES = 512


def step_kernel(
    plen_h, tok_h, ngain_h, w_up_h, w_down_h, fgain_h, w_proj_h, quer_h, assign_h, valid_h,
    up_h, down_h, proj_h, qg_h,
    plen, tok, ngain, w_up, w_down, fgain, w_proj, quer, assign, valid,
    nrm, gd, cs, cr, xs, xr, ys, yr, lo, wfull, frow, psend, prow, allf, vcol, score, sgrad, qg,
    fcs, fcr, ts, tr, rsend, rgot, grow, pj, pjf, og, h_t, n_t,
    ds, dyr, dz, dr, us, uyr, uz, ur, up_v, down_v, proj_v,
    load_sems, store_sems, send_sems, recv_sems,
):
    me = Place()
    send = Sends(send_sems, recv_sems)
    core, chip, x, y, t, z, yl = me.core, me.chip, me.x, me.y, me.t, me.z, me.yl
    me.greet()
    loads = {}
    for n, (name, src, dst) in enumerate((
        ("tok", tok_h, tok), ("ngain", ngain_h, ngain), ("w_up", w_up_h, w_up), ("w_down", w_down_h, w_down),
        ("w_proj", w_proj_h, w_proj), ("plen", plen_h, plen), ("fgain", fgain_h, fgain),
        ("quer", quer_h, quer), ("assign", assign_h, assign), ("valid", valid_h, valid),
    )):
        loads[name] = pltpu.make_async_copy(src, dst, load_sems.at[n])
        loads[name].start()
    stores = []

    def store(src, dst):
        copy = pltpu.make_async_copy(src, dst, store_sems.at[len(stores)])
        copy.start()
        stores.append(copy)

    loads["tok"].wait()
    loads["ngain"].wait()
    tokens = tok[...].astype(F32)
    centred = tokens - jnp.mean(tokens, axis=1, keepdims=True)
    variance = jnp.mean(centred * centred, axis=1, keepdims=True)
    normed = (centred * lax.rsqrt(variance + EPS) * ngain[...]).astype(BF16)
    nrm[...] = normed
    loads["w_up"].wait()
    pre = dot(normed, w_up[...])
    tanh = jnp.tanh(GC * (pre + GA * pre * pre * pre))
    hidden = (0.5 * pre * (1.0 + tanh)).astype(BF16)
    gd[...] = 0.5 * (1.0 + tanh) + 0.5 * pre * (1.0 - tanh * tanh) * (GC * (1.0 + 3.0 * GA * pre * pre))
    loads["w_proj"].wait()
    loads["w_down"].wait()
    wfull[y, x, core] = w_proj[...]
    for j in range(2):
        cs[j] = dot(hidden, w_down[:, at((1 - core) * 2 + j, 512)]).astype(BF16)
    me.met()
    to_core = [send(cs.at[j], cr.at[j], me.other_core()) for j in range(2)]
    w_y = [send(w_proj, wfull.at[y, x, core], me.along_y(i)) for i in (1, 2, 3)]
    to_x = []
    for j in range(2):
        own = dot(hidden, w_down[:, at(core * 2 + j, 512)])
        to_core[j].wait_recv()
        xs[j] = (own + cr[j].astype(F32)).astype(BF16).reshape(4, 4, 16, 512)
        to_x.append(
            [send(xs.at[j, :, lax.rem(x + i, 4)], xr.at[j, i - 1], me.along_x(i)) for i in (2, 1, 3)]
        )
    h_t[...] = hidden.T
    for name in ("plen", "fgain", "quer", "assign", "valid"):
        loads[name].wait()
    vcol[...] = jnp.broadcast_to(valid[...].astype(F32), (128, 256)).T
    for copy in w_y:
        copy.wait_recv()
    to_y = []
    for j in range(2):
        for copy in to_x[j]:
            copy.wait_recv()
        total = xs[j, :, x].astype(F32)
        for i in range(3):
            total += xr[j, i].astype(F32)
        ys[j] = total.astype(BF16)
        to_y.append([send(ys.at[j, lax.rem(y + i, 4)], yr.at[j, i - 1], me.along_y(i)) for i in (2, 1, 3)])
    w_x = [send(wfull.at[:, x, core], wfull.at[:, x, core], me.along_x(i)) for i in (1, 2, 3)]
    for j in range(2):
        for copy in to_y[j]:
            copy.wait_recv()
        total = ys[j, y].astype(F32)
        for i in range(3):
            total += yr[j, i].astype(F32)
        lo[core, :, j * 512 : (j + 1) * 512] = total
    half = send(lo.at[core], lo.at[core], me.other_core())
    for copy in w_x:
        copy.wait_recv()
    w_core = send(wfull.at[:, :, core], wfull.at[:, :, core], me.other_core())
    half.wait_recv()
    layer_out = tok[at(chip, 16), :].astype(F32) + jnp.concatenate([lo[0], lo[1]], axis=1)
    centred = layer_out - jnp.mean(layer_out, axis=1, keepdims=True)
    inv_scale = lax.rsqrt(jnp.mean(centred * centred, axis=1, keepdims=True) + EPS)
    out_hat = centred * inv_scale
    final = out_hat * fgain[...]
    pool_weight = pool_weights(plen, chip)
    pooled = jnp.sum(final * pool_weight, axis=0, keepdims=True)
    pooled_low = pooled.astype(BF16)
    w_core.wait_recv()
    feat = dot(jnp.broadcast_to(pooled_low, (16, 2048)), wfull[...].reshape(2048, 256))
    frow[chip] = feat[:1].astype(BF16).astype(F32)
    to_plane = [send(frow.at[chip], frow.at[chip], me.in_plane(i)) for i in range(1, 16)]
    rounded = pooled_low.astype(F32)
    for k in range(16):
        psend[k] = rounded[:, k * 128 : (k + 1) * 128]
    prow[chip] = psend[chip]
    pooled_to = [send(psend.at[lax.rem(chip + i, 16)], prow.at[chip], me.in_plane(i)) for i in range(1, 16)]
    n_t[...] = nrm[...].T
    for copy in to_plane:
        copy.wait_recv()
    allf[t] = jnp.concatenate([frow[k] for k in range(16)], axis=0).astype(BF16)
    to_text = [send(allf.at[t], allf.at[t], me.in_text(i)) for i in range(1, 16)]
    for copy in pooled_to:
        copy.wait_recv()
    pj[t, :, 256:] = jnp.concatenate([prow[k] for k in range(16)], axis=0).astype(BF16)
    for copy in to_text:
        copy.wait_recv()

    features = allf[...].reshape(256, 256)
    score[...] = dot(features, quer[...], ((1,), (1,)))
    chosen = assign[...]

    @pl.loop(0, 16)
    def _(r):
        spot = at(r, 16)
        s = score[spot, :] * SCORE_SCALE + LOGIT_BIAS
        concept = lax.broadcasted_iota(jnp.int32, (16, 1100), 0) + r * 16
        hit = concept == chosen
        u = jnp.where(hit, -s, s)
        e = jnp.exp(-jnp.abs(u))
        more = 1.0 / (1.0 + e)
        less = e * more
        p = jnp.where(u >= 0.0, more, less)
        q = jnp.where(u >= 0.0, less, more)
        soft = jnp.maximum(u, 0.0) + jnp.log1p(e)
        factor = jnp.where(hit, -ALPHA, 1.0 - ALPHA) * vcol[spot, :1]
        sgrad[spot, :] = (factor * p * p * (p + 2.0 * q * soft)).astype(BF16)

    terms = dot(sgrad[...], quer[...]) * (SCORE_SCALE / IMAGES)
    halves = (terms[:, :128], terms[:, 128:])
    mine = jnp.where(core == 0, halves[0], halves[1])
    fcs[...] = jnp.where(core == 0, halves[1], halves[0]).astype(BF16)
    to_core = send(fcs, fcr, me.other_core())
    to_core.wait_recv()
    ts[...] = (mine + fcr[...].astype(F32)).astype(BF16).reshape(16, 16, 128)
    to_text2 = [send(ts.at[lax.rem(t + i, 16)], tr.at[i - 1], me.in_text(i)) for i in range(1, 16)]
    query_grad = dot(sgrad[...], features, ((0,), (0,))) * SCORE_SCALE
    qg[pl.ds(0, 1100, stride=2), :] = query_grad[:, :128]
    qg[pl.ds(1, 1100, stride=2), :] = query_grad[:, 128:]
    store(qg, qg_h)
    total = ts[t].astype(F32)
    for i in range(15):
        to_text2[i].wait_recv()
        total += tr[i].astype(F32)
    for k in range(16):
        rsend[k] = total[k : k + 1]
    rgot[core, chip] = rsend[chip]
    to_rows = [send(rsend.at[chip], rgot.at[core, chip], me.other_core())]
    for i in range(1, 16):
        there = rsend.at[lax.rem(chip + i, 16)]
        to_rows.append(send(there, rgot.at[core, chip], me.in_plane(i)))
        to_rows.append(send(there, rgot.at[core, chip], me.in_plane(i, 1)))
    for copy in to_rows:
        copy.wait_recv()
    sums = []
    for c in range(2):
        total = rgot[c, 0]
        for k in range(1, 16):
            total += rgot[c, k]
        sums.append(total)
    row = jnp.concatenate(sums, axis=1)
    grow[chip] = row
    high = row.astype(BF16).astype(F32)
    middle = (row - high).astype(BF16).astype(F32)
    low = row - high - middle
    part = lax.broadcasted_iota(jnp.int32, (16, 256), 0)
    rows = jnp.where(part == 0, high, jnp.where(part == 1, middle, jnp.where(part == 2, low, 0.0)))
    pooled_grad = jnp.sum(
        dot(rows.astype(BF16), wfull[...].reshape(2048, 256), ((1,), (1,))), axis=0, keepdims=True
    )
    hat = pooled_grad * fgain[...]
    first = jnp.mean(hat, axis=1, keepdims=True)
    second = jnp.mean(hat * out_hat, axis=1, keepdims=True)
    out_grad = ((hat - first - out_hat * second) * (pool_weight * inv_scale)).astype(BF16)
    og[0, y, x] = out_grad[:, :1024]
    og[1, y, x] = out_grad[:, 1024:]
    own = og.at[core, y, x]
    to_y = [send(own, own, me.along_y(i)) for i in (2, 1, 3)]
    waves = [[send(own, own, me.along_x(i)) for i in (2, 1, 3)]]
    to_grow = [send(grow.at[chip], grow.at[chip], me.in_plane(i)) for i in range(1, 16)]
    to_other = []
    for copy, i in ((to_y[1], 1), (to_y[2], 3), (to_y[0], 2)):
        copy.wait_recv()
        block = og.at[core, lax.rem(y + 4 - i, 4), x]
        waves.append([send(block, block, me.along_x(j)) for j in (2, 1, 3)])
        to_other.append(send(block, block, me.other_core()))
    for copy in to_grow:
        copy.wait_recv()
    pj[t, :, :256] = jnp.concatenate([grow[k] for k in range(16)], axis=0).astype(BF16)
    pj_to = [send(pj.at[t], pj.at[t], me.in_text(i)) for i in range(1, 16)]
    for wave, i in zip(waves, (0, 1, 3, 2)):
        for copy, j in zip(wave, (2, 1, 3)):
            copy.wait_recv()
            block = og.at[core, lax.rem(y + 4 - i, 4), lax.rem(x + 4 - j, 4)]
            to_other.append(send(block, block, me.other_core()))
    for copy in to_other:
        copy.wait_recv()
    order = (4, 3, 5, 2, 6, 1, 7, 0)

    def exchange(parts, arrived):
        copies = {}
        for i in order:
            spot = lax.rem(z + i, 8)
            copies[i] = send(parts.at[spot, 1 - yl], arrived.at[i], me.across())
        return copies

    def onward(copies, parts, arrived, staged, landed):
        copies_z = {}
        for i in order[:-1]:
            copies[i].wait_recv()
            staged[i - 1] = (parts[lax.rem(z + i, 8), yl].astype(F32) + arrived[i].astype(F32)).astype(BF16)
            copies_z[i] = send(staged.at[i - 1], landed.at[i - 1], me.along_z(i))
        return copies_z

    def finish(copies, copies_z, parts, arrived, landed, out):
        copies[0].wait_recv()
        total = parts[z, yl].astype(F32) + arrived[0].astype(F32)
        for i in (1, 7, 2, 6, 3, 5, 4):
            copies_z[i].wait_recv()
            total += landed[i - 1].astype(F32)
        out[...] = total

    halves = [og[h].reshape(256, 1024) for h in range(2)]
    for h in range(2):
        product = dot(h_t[...], halves[h]).astype(BF16)
        for k in range(8):
            ds[h * 4 + k // 2, k % 2] = product[:, k * 128 : (k + 1) * 128]
    down_y = exchange(ds, dyr)
    hidden_grad = dot(halves[0], w_down[:, :1024], ((1,), (1,))) + dot(halves[1], w_down[:, 1024:], ((1,), (1,)))
    pre_grad = (hidden_grad * gd[...]).astype(BF16)
    us[...] = dot(n_t[...], pre_grad).astype(BF16).reshape(8, 2, 128, 256)
    up_y = exchange(us, uyr)
    down_z = onward(down_y, ds, dyr, dz, dr)
    up_z = onward(up_y, us, uyr, uz, ur)
    for copy in pj_to:
        copy.wait_recv()
    pjf[...] = dot(pj[:, :, 256:].reshape(256, 128), pj[:, :, :256].reshape(256, 256), ((0,), (0,)))
    proj_v[...] = pjf[at(core, 64), :]
    store(proj_v, proj_h)
    finish(down_y, down_z, ds, dyr, dr, down_v)
    store(down_v, down_h)
    finish(up_y, up_z, us, uyr, ur, up_v)
    store(up_v, up_h)
    send.drain()
    for copy in stores:
        copy.wait()


def step(*args):
    anywhere = pl.BlockSpec(memory_space=pl.ANY)
    return pl.pallas_call(
        step_kernel,
        name="step",
        in_specs=[anywhere] * 10,
        out_specs=[anywhere] * 4,
        out_shape=(
            jax.ShapeDtypeStruct((128, 256), F32),
            jax.ShapeDtypeStruct((256, 128), F32),
            jax.ShapeDtypeStruct((64, 256), F32),
            jax.ShapeDtypeStruct((2200, 128), F32),
        ),
        scratch_shapes=[
            pltpu.VMEM((1, 16), jnp.int32),
            pltpu.VMEM((256, 2048), BF16),
            pltpu.VMEM((1, 2048), F32),
            pltpu.VMEM((2048, 256), BF16),
            pltpu.VMEM((256, 2048), BF16),
            pltpu.VMEM((1, 2048), F32),
            pltpu.VMEM((64, 256), BF16),
            pltpu.VMEM((1100, 256), BF16),
            pltpu.VMEM((1, 1100), jnp.int32),
            pltpu.VMEM((1, 256), jnp.int32),
            pltpu.VMEM((256, 2048), BF16),
            pltpu.VMEM((256, 256), F32),
            pltpu.VMEM((2, 256, 512), BF16),
            pltpu.VMEM((2, 256, 512), BF16),
            pltpu.VMEM((2, 4, 4, 16, 512), BF16),
            pltpu.VMEM((2, 3, 4, 16, 512), BF16),
            pltpu.VMEM((2, 4, 16, 512), BF16),
            pltpu.VMEM((2, 3, 16, 512), BF16),
            pltpu.VMEM((2, 16, 1024), F32),
            pltpu.VMEM((4, 4, 2, 64, 256), BF16),
            pltpu.VMEM((16, 1, 256), F32),
            pltpu.VMEM((16, 1, 128), F32),
            pltpu.VMEM((16, 1, 128), F32),
            pltpu.VMEM((16, 16, 256), BF16),
            pltpu.VMEM((256, 128), F32),
            pltpu.VMEM((256, 1100), F32),
            pltpu.VMEM((256, 1100), BF16),
            pltpu.VMEM((2200, 128), F32),
            pltpu.VMEM((256, 128), BF16),
            pltpu.VMEM((256, 128), BF16),
            pltpu.VMEM((16, 16, 128), BF16),
            pltpu.VMEM((15, 16, 128), BF16),
            pltpu.VMEM((16, 1, 128), F32),
            pltpu.VMEM((2, 16, 1, 128), F32),
            pltpu.VMEM((16, 1, 256), F32),
            pltpu.VMEM((16, 16, 384), BF16),
            pltpu.VMEM((128, 256), F32),
            pltpu.VMEM((2, 4, 4, 16, 1024), BF16),
            pltpu.VMEM((256, 256), BF16),
            pltpu.VMEM((2048, 256), BF16),
            pltpu.VMEM((8, 2, 256, 128), BF16),
            pltpu.VMEM((8, 256, 128), BF16),
            pltpu.VMEM((7, 256, 128), BF16),
            pltpu.VMEM((7, 256, 128), BF16),
            pltpu.VMEM((8, 2, 128, 256), BF16),
            pltpu.VMEM((8, 128, 256), BF16),
            pltpu.VMEM((7, 128, 256), BF16),
            pltpu.VMEM((7, 128, 256), BF16),
            pltpu.VMEM((128, 256), F32),
            pltpu.VMEM((256, 128), F32),
            pltpu.VMEM((64, 256), F32),
            pltpu.SemaphoreType.DMA((10,)),
            pltpu.SemaphoreType.DMA((4,)),
            pltpu.SemaphoreType.DMA((COPIES,)),
            pltpu.SemaphoreType.DMA((COPIES,)),
        ],
        compiler_params=pltpu.CompilerParams(
            collective_id=0, has_side_effects=True, vmem_limit_bytes=62 << 20
        ),
    )(*args)


def body(
    prompt_embeds, prompt_len, norm_gain, w_up, w_down, final_gain, w_proj, queries, assign, valid
):
    up_grad, down_grad, proj_grad, query_grad = step(
        prompt_len.reshape(1, 16),
        prompt_embeds.reshape(256, 2048),
        norm_gain.reshape(1, 2048),
        w_up,
        w_down,
        final_gain.reshape(1, 2048),
        w_proj,
        queries.reshape(1100, 256),
        assign,
        valid,
    )
    return (up_grad, down_grad, proj_grad, query_grad.reshape(1, 1100, 256))


def solution(mesh):
    return jax.shard_map(
        body,
        mesh=mesh,
        in_specs=(
            P("text", None, None),
            P("text"),
            P(),
            P(None, "det"),
            P("det", None),
            P(),
            P("det", None),
            P(("text", "det"), None, None),
            P(("text", "det"), None),
            P(("text", "det"), None),
        ),
        out_specs=(
            P("text", "det"),
            P("det", "text"),
            P("det", None),
            P(("text", "det"), None, None),
        ),
        check_vma=False,
    )
```

time: 136 us -> 116 us (0.85)
  local copies, waits for them, and re-layouts: 15 us -> 7.26 us
  Pallas kernels: 113 us -> 108 us
  matrix products: 4.43 us -> 0 us
  other arithmetic: 1.45 us -> 0 us
    unnamed x22 -> x4, local copies, waits for them, and re-layouts: 15 us -> 7.26 us
    pallas_call x2 -> x1, Pallas kernels: 113 us -> 108 us  [step(): pl.pallas_call(step_kernel, name='step', in_specs=[anywhere] * 10, out_sp...]
    dot_general x3 -> x0, matrix products: 4.43 us -> none  [dot(): return lax.dot_general(a, b, (dims, ((), ())), preferred_element_type=F32)]
where the time goes in v2:
time: 116 us
  Pallas kernels  108 us (93%)
  local copies, waits for them, and re-layouts  7.26 us (6%)
    pallas_call x1, Pallas kernels, step(): pl.pallas_call(step_kernel, name='step', in_specs=[anywhere] * 10, out_sp...  108 us
    unnamed x4, local copies, waits for them, and re-layouts  7.26 us

profile of v2, /device:TPU:1, one launch (start us, length us, event | category | flops | bytes accessed | tf_op | source)
XLA Modules:
  0.0 116.1 jit_solution(345849292218528943)
XLA Ops:
  0.6 108.2 %step.1 = (f32[128,256]{1,0:T(8,128)}, f32[256,128]{1,0:T(8,128)}, f32[64,256]{1,0:T(8,128)}, f32[2200,128]{1,0:T(8,128)}) custom-call(s32[1,16]{1,0:T(1,128)} %bitcast.11, bf16[256,2048]{1,0:T(8,128)(2,1)} %bitcast.7, f32[1,2048]{1,0:T(1,128)} %bitcast.9, bf16[2048,256]{1,0:T(8,128)(2,1)} %w_up_h.1, bf16[256,2048]{1,0:T(8,128)(2,1)} %w_down_h.1, ...), custom_call_target="tpu_custom_call" | custom-call | tf_op jit(solution)/shard_map/step/pallas_call | solution.py:361
  108.8 1.6 %copy.20 = f32[128,256]{1,0:T(8,128)} copy(f32[128,256]{1,0:T(8,128)} %get-tuple-element.24) | data formatting | bytes 262144
  110.4 1.6 %copy.21 = f32[256,128]{1,0:T(8,128)} copy(f32[256,128]{1,0:T(8,128)} %get-tuple-element.25) | data formatting | bytes 262144
  111.9 1.5 %copy.22 = f32[64,256]{1,0:T(8,128)} copy(f32[64,256]{1,0:T(8,128)} %get-tuple-element.26) | data formatting | bytes 131072
  113.4 2.6 %copy.23 = f32[1,1100,256]{2,0,1:T(1,128)} copy(f32[1,1100,256]{2,0,1:T(1,128)} %bitcast.6) | data formatting | bytes 2252800

commit v3 on v2

--- a/solution.py
+++ b/solution.py
@@ -99,7 +99,7 @@
     return jnp.where(slot < length, 1.0 / length, 0.0)
 
 
-COPIES = 2 + 3 + 6 + 6 + 3 + 1 + 1 + 15 + 15 + 15 + 1 + 15 + 31 + 15 + 15 + 3 + 12 + 15 + 30
+COPIES = 2 + 3 + 6 + 6 + 3 + 1 + 1 + 15 + 15 + 15 + 1 + 15 + 31 + 15 + 15 + 3 + 12 + 15 + 15 + 7 + 7 + 3 + 12 + 16 + 1
 SCORE_SCALE = 256 ** (-0.5)
 IMAGES = 512
 
@@ -108,10 +108,9 @@
     plen_h, tok_h, ngain_h, w_up_h, w_down_h, fgain_h, w_proj_h, quer_h, assign_h, valid_h,
     up_h, down_h, proj_h, qg_h,
     plen, tok, ngain, w_up, w_down, fgain, w_proj, quer, assign, valid,
-    nrm, gd, cs, cr, xs, xr, ys, yr, lo, wfull, frow, psend, prow, allf, vcol, score, sgrad, qg,
-    fcs, fcr, ts, tr, rsend, rgot, grow, pj, pjf, og, h_t, n_t,
-    ds, dyr, dz, dr, us, uyr, uz, ur, up_v, down_v, proj_v,
-    load_sems, store_sems, send_sems, recv_sems,
+    nrm, gd, cs, cr, xs, xr, ys, yr, lo, wfull, frow, psend, prow, allf, vcol, score, sgrad, qg, up_o, down_o, proj_o,
+    fcs, fcr, ts, tr, rsend, rgot, grow, pj, pjf, og, h_all, n_t, ogz, dg, dp, dpr,
+    us, uyr, uz, ur, load_sems, store_sems, send_sems, recv_sems,
 ):
     me = Place()
     send = Sends(send_sems, recv_sems)
@@ -149,6 +148,7 @@
     wfull[y, x, core] = w_proj[...]
     for j in range(2):
         cs[j] = dot(hidden, w_down[:, at((1 - core) * 2 + j, 512)]).astype(BF16)
+    h_all[z] = hidden.T
     me.met()
     to_core = [send(cs.at[j], cr.at[j], me.other_core()) for j in range(2)]
     w_y = [send(w_proj, wfull.at[y, x, core], me.along_y(i)) for i in (1, 2, 3)]
@@ -160,7 +160,7 @@
         to_x.append(
             [send(xs.at[j, :, lax.rem(x + i, 4)], xr.at[j, i - 1], me.along_x(i)) for i in (2, 1, 3)]
         )
-    h_t[...] = hidden.T
+    h_to = [send(h_all.at[z], h_all.at[z], me.along_z(i)) for i in (4, 3, 5, 2, 6, 1, 7)]
     for name in ("plen", "fgain", "quer", "assign", "valid"):
         loads[name].wait()
     vcol[...] = jnp.broadcast_to(valid[...].astype(F32), (128, 256)).T
@@ -287,82 +287,132 @@
     own = og.at[core, y, x]
     to_y = [send(own, own, me.along_y(i)) for i in (2, 1, 3)]
     waves = [[send(own, own, me.along_x(i)) for i in (2, 1, 3)]]
+    for k in range(16):
+        ogz[k] = out_grad[:, 128 * k : 128 * k + 128]
+    dg[core, y, x, z] = ogz[2 * z + core]
+    z_to = [
+        send(ogz.at[lax.rem(z + i, 8) * 2 + core], dg.at[core, y, x, z], me.along_z(i))
+        for i in (4, 3, 5, 2, 6, 1, 7)
+    ]
     to_grow = [send(grow.at[chip], grow.at[chip], me.in_plane(i)) for i in range(1, 16)]
+
+    def spread_y(to_y, buf, waves, to_other):
+        for copy, i in ((to_y[1], 1), (to_y[2], 3), (to_y[0], 2)):
+            copy.wait_recv()
+            block = buf.at[core, lax.rem(y + 4 - i, 4), x]
+            waves.append([send(block, block, me.along_x(j)) for j in (2, 1, 3)])
+            to_other.append(send(block, block, me.other_core()))
+
+    def spread_x(buf, waves, to_other):
+        for wave, i in zip(waves, (0, 1, 3, 2)):
+            for copy, j in zip(wave, (2, 1, 3)):
+                copy.wait_recv()
+                block = buf.at[core, lax.rem(y + 4 - i, 4), lax.rem(x + 4 - j, 4)]
+                to_other.append(send(block, block, me.other_core()))
+
     to_other = []
-    for copy, i in ((to_y[1], 1), (to_y[2], 3), (to_y[0], 2)):
-        copy.wait_recv()
-        block = og.at[core, lax.rem(y + 4 - i, 4), x]
-        waves.append([send(block, block, me.along_x(j)) for j in (2, 1, 3)])
-        to_other.append(send(block, block, me.other_core()))
+    spread_y(to_y, og, waves, to_other)
+    for copy in z_to:
+        copy.wait_recv()
+    own = dg.at[core, y, x]
+    dg_y = [send(own, own, me.along_y(i)) for i in (2, 1, 3)]
+    dg_waves = [[send(own, own, me.along_x(i)) for i in (2, 1, 3)]]
+    dg_other = [send(own, own, me.other_core())]
     for copy in to_grow:
         copy.wait_recv()
     pj[t, :, :256] = jnp.concatenate([grow[k] for k in range(16)], axis=0).astype(BF16)
     pj_to = [send(pj.at[t], pj.at[t], me.in_text(i)) for i in range(1, 16)]
-    for wave, i in zip(waves, (0, 1, 3, 2)):
-        for copy, j in zip(wave, (2, 1, 3)):
-            copy.wait_recv()
-            block = og.at[core, lax.rem(y + 4 - i, 4), lax.rem(x + 4 - j, 4)]
-            to_other.append(send(block, block, me.other_core()))
+    spread_x(og, waves, to_other)
+    spread_y(dg_y, dg, dg_waves, dg_other)
     for copy in to_other:
         copy.wait_recv()
-    order = (4, 3, 5, 2, 6, 1, 7, 0)
-
-    def exchange(parts, arrived):
-        copies = {}
-        for i in order:
-            spot = lax.rem(z + i, 8)
-            copies[i] = send(parts.at[spot, 1 - yl], arrived.at[i], me.across())
-        return copies
-
-    def onward(copies, parts, arrived, staged, landed):
-        copies_z = {}
-        for i in order[:-1]:
-            copies[i].wait_recv()
-            staged[i - 1] = (parts[lax.rem(z + i, 8), yl].astype(F32) + arrived[i].astype(F32)).astype(BF16)
-            copies_z[i] = send(staged.at[i - 1], landed.at[i - 1], me.along_z(i))
-        return copies_z
-
-    def finish(copies, copies_z, parts, arrived, landed, out):
-        copies[0].wait_recv()
-        total = parts[z, yl].astype(F32) + arrived[0].astype(F32)
-        for i in (1, 7, 2, 6, 3, 5, 4):
-            copies_z[i].wait_recv()
-            total += landed[i - 1].astype(F32)
-        out[...] = total
-
     halves = [og[h].reshape(256, 1024) for h in range(2)]
-    for h in range(2):
-        product = dot(h_t[...], halves[h]).astype(BF16)
-        for k in range(8):
-            ds[h * 4 + k // 2, k % 2] = product[:, k * 128 : (k + 1) * 128]
-    down_y = exchange(ds, dyr)
     hidden_grad = dot(halves[0], w_down[:, :1024], ((1,), (1,))) + dot(halves[1], w_down[:, 1024:], ((1,), (1,)))
     pre_grad = (hidden_grad * gd[...]).astype(BF16)
     us[...] = dot(n_t[...], pre_grad).astype(BF16).reshape(8, 2, 128, 256)
-    up_y = exchange(us, uyr)
-    down_z = onward(down_y, ds, dyr, dz, dr)
-    up_z = onward(up_y, us, uyr, uz, ur)
+    order = (4, 3, 5, 2, 6, 1, 7, 0)
+    up_y, up_z = {}, {}
+    for i in order:
+        up_y[i] = send(us.at[lax.rem(z + i, 8), 1 - yl], uyr.at[i], me.across())
+
+    def onward(i):
+        up_y[i].wait_recv()
+        uz[i - 1] = (us[lax.rem(z + i, 8), yl].astype(F32) + uyr[i].astype(F32)).astype(BF16)
+        up_z[i] = send(uz.at[i - 1], ur.at[i - 1], me.along_z(i))
+
+    for i in order[:4]:
+        onward(i)
+    spread_x(dg, dg_waves, dg_other)
+    for i in order[4:6]:
+        onward(i)
+    for copy in dg_other + h_to:
+        copy.wait_recv()
+
+    def down_product(h):
+        total = dot(h_all[0], dg[h, :, :, 0].reshape(256, 128))
+        for k in range(1, 8):
+            total += dot(h_all[k], dg[h, :, :, k].reshape(256, 128))
+        return total
+
+    dp[...] = down_product(1 - yl).astype(BF16)
+    dp_to = send(dp, dpr, me.across())
+    onward(order[6])
+    down_own = down_product(yl)
     for copy in pj_to:
         copy.wait_recv()
     pjf[...] = dot(pj[:, :, 256:].reshape(256, 128), pj[:, :, :256].reshape(256, 256), ((0,), (0,)))
-    proj_v[...] = pjf[at(core, 64), :]
-    store(proj_v, proj_h)
-    finish(down_y, down_z, ds, dyr, dr, down_v)
-    store(down_v, down_h)
-    finish(up_y, up_z, us, uyr, ur, up_v)
-    store(up_v, up_h)
+    proj_o[...] = pjf[at(core, 64), :]
+    store(proj_o, proj_h)
+    dp_to.wait_recv()
+    down_o[...] = down_own + dpr[...].astype(F32)
+    store(down_o, down_h)
+    up_y[0].wait_recv()
+    total = us[z, yl].astype(F32) + uyr[0].astype(F32)
+    for i in (4, 3, 5, 2, 6, 1, 7):
+        up_z[i].wait_recv()
+        total += ur[i - 1].astype(F32)
+    up_o[...] = total
+    store(up_o, up_h)
     send.drain()
     for copy in stores:
         copy.wait()
 
 
+def hand_out_kernel(a, b, c, d, a_o, b_o, c_o, d_o, a_v, b_v, c_v, d_v, sems):
+    parts = []
+    for lo, n in ((0, 552), (552, 552), (1104, 552), (1656, 544)):
+        rows = pl.ds(lo, n)
+        parts.append((d.at[rows], d_v.at[rows], d_o.at[rows]))
+    parts += [(a, a_v, a_o), (b, b_v, b_o), (c, c_v, c_o)]
+    loads = [pltpu.make_async_copy(src, mid, sems.at[0, n]) for n, (src, mid, _) in enumerate(parts)]
+    stores = [pltpu.make_async_copy(mid, dst, sems.at[1, n]) for n, (_, mid, dst) in enumerate(parts)]
+    for load in loads:
+        load.start()
+    for load, store in zip(loads, stores):
+        load.wait()
+        store.start()
+    for store in stores:
+        store.wait()
+
+
+def hand_out(arrays):
+    return pl.pallas_call(
+        hand_out_kernel,
+        name="hand_out",
+        in_specs=[pl.BlockSpec(memory_space=pltpu.HBM)] * 4,
+        out_specs=[pl.BlockSpec(memory_space=pltpu.HBM)] * 4,
+        out_shape=[jax.ShapeDtypeStruct(a.shape, a.dtype) for a in arrays],
+        scratch_shapes=[pltpu.VMEM(a.shape, a.dtype) for a in arrays] + [pltpu.SemaphoreType.DMA((2, 7))],
+        compiler_params=pltpu.CompilerParams(vmem_limit_bytes=62 << 20),
+    )(*arrays)
+
+
 def step(*args):
-    anywhere = pl.BlockSpec(memory_space=pl.ANY)
     return pl.pallas_call(
         step_kernel,
         name="step",
-        in_specs=[anywhere] * 10,
-        out_specs=[anywhere] * 4,
+        in_specs=[pl.BlockSpec(memory_space=pltpu.HBM)] * 10,
+        out_specs=[pl.BlockSpec(memory_space=pltpu.HBM)] * 4,
         out_shape=(
             jax.ShapeDtypeStruct((128, 256), F32),
             jax.ShapeDtypeStruct((256, 128), F32),
@@ -398,6 +448,9 @@
             pltpu.VMEM((256, 1100), F32),
             pltpu.VMEM((256, 1100), BF16),
             pltpu.VMEM((2200, 128), F32),
+            pltpu.VMEM((128, 256), F32),
+            pltpu.VMEM((256, 128), F32),
+            pltpu.VMEM((64, 256), F32),
             pltpu.VMEM((256, 128), BF16),
             pltpu.VMEM((256, 128), BF16),
             pltpu.VMEM((16, 16, 128), BF16),
@@ -408,19 +461,16 @@
             pltpu.VMEM((16, 16, 384), BF16),
             pltpu.VMEM((128, 256), F32),
             pltpu.VMEM((2, 4, 4, 16, 1024), BF16),
-            pltpu.VMEM((256, 256), BF16),
+            pltpu.VMEM((8, 256, 256), BF16),
             pltpu.VMEM((2048, 256), BF16),
-            pltpu.VMEM((8, 2, 256, 128), BF16),
-            pltpu.VMEM((8, 256, 128), BF16),
-            pltpu.VMEM((7, 256, 128), BF16),
-            pltpu.VMEM((7, 256, 128), BF16),
+            pltpu.VMEM((16, 16, 128), BF16),
+            pltpu.VMEM((2, 4, 4, 8, 16, 128), BF16),
+            pltpu.VMEM((256, 128), BF16),
+            pltpu.VMEM((256, 128), BF16),
             pltpu.VMEM((8, 2, 128, 256), BF16),
             pltpu.VMEM((8, 128, 256), BF16),
             pltpu.VMEM((7, 128, 256), BF16),
             pltpu.VMEM((7, 128, 256), BF16),
-            pltpu.VMEM((128, 256), F32),
-            pltpu.VMEM((256, 128), F32),
-            pltpu.VMEM((64, 256), F32),
             pltpu.SemaphoreType.DMA((10,)),
             pltpu.SemaphoreType.DMA((4,)),
             pltpu.SemaphoreType.DMA((COPIES,)),
@@ -435,7 +485,7 @@
 def body(
     prompt_embeds, prompt_len, norm_gain, w_up, w_down, final_gain, w_proj, queries, assign, valid
 ):
-    up_grad, down_grad, proj_grad, query_grad = step(
+    results = step(
         prompt_len.reshape(1, 16),
         prompt_embeds.reshape(256, 2048),
         norm_gain.reshape(1, 2048),
@@ -447,6 +497,7 @@
         assign,
         valid,
     )
+    up_grad, down_grad, proj_grad, query_grad = hand_out(results)
     return (up_grad, down_grad, proj_grad, query_grad.reshape(1, 1100, 256))
 
 

time: 116 us -> 102 us (0.88)
  local copies, waits for them, and re-layouts: 7.26 us -> 0 us
  Pallas kernels: 108 us -> 101 us
    unnamed x4 -> x0, local copies, waits for them, and re-layouts: 7.26 us -> none
    pallas_call x1 -> x2, Pallas kernels: 108 us -> 101 us  [the longest x1 98.9 us: step(): pl.pallas_call(step_kernel, name='step', in_specs=[pl.BlockSpec(memory_sp...]
where the time goes in v3:
time: 102 us
  Pallas kernels  101 us (99%)
    pallas_call x1, Pallas kernels, step(): pl.pallas_call(step_kernel, name='step', in_specs=[pl.BlockSpec(memory_sp...  98.9 us
    pallas_call x1, Pallas kernels, hand_out(): pl.pallas_call(hand_out_kernel, name='hand_out', in_specs=[pl.BlockSpec(m...  2.17 us

profile of v3, /device:TPU:1, one launch (start us, length us, event | category | flops | bytes accessed | tf_op | source)
XLA Modules:
  0.0 101.7 jit_solution(7693281944935781987)
XLA Ops:
  0.6 98.9 %step.1 = (f32[128,256]{1,0:T(8,128)}, f32[256,128]{1,0:T(8,128)}, f32[64,256]{1,0:T(8,128)}, f32[2200,128]{1,0:T(8,128)}) custom-call(s32[1,16]{1,0:T(1,128)} %bitcast.10, bf16[256,2048]{1,0:T(8,128)(2,1)} %bitcast.6, f32[1,2048]{1,0:T(1,128)} %bitcast.8, bf16[2048,256]{1,0:T(8,128)(2,1)} %w_up_h.1, bf16[256,2048]{1,0:T(8,128)(2,1)} %w_down_h.1, ...), custom_call_target="tpu_custom_call" | custom-call | tf_op jit(solution)/shard_map/step/pallas_call | solution.py:411
  99.5 2.2 %hand_out.1 = (f32[128,256]{1,0:T(8,128)}, f32[256,128]{1,0:T(8,128)}, f32[64,256]{1,0:T(8,128)}, f32[2200,128]{1,0:T(8,128)}) custom-call(f32[128,256]{1,0:T(8,128)} %get-tuple-element.12.a, f32[256,128]{1,0:T(8,128)} %get-tuple-element.13.b, f32[64,256]{1,0:T(8,128)} %get-tuple-element.14.c, f32[2200,128]{1,0:T(8,128)} %get-tuple-element.15.d), custom_call_target="tpu_custom_call" | custom-call | tf_op jit(solution)/shard_map/hand_out/pallas_call | solution.py:399

commit v4 on v3

--- a/solution.py
+++ b/solution.py
@@ -35,9 +35,8 @@
     def along_y(self, i):
         return {"det": (lax.rem(self.y + i, 4) * 4 + self.x) * 2 + self.core}
 
-    def in_plane(self, i, swap=0):
-        core = 1 - self.core if swap else self.core
-        return {"det": lax.rem(self.chip + i, 16) * 2 + core}
+    def in_plane(self, i):
+        return {"det": lax.rem(self.chip + i, 16) * 2 + self.core}
 
     def in_text(self, i):
         return {"text": lax.rem(self.t + i, 16)}
@@ -53,11 +52,10 @@
         pl.semaphore_signal(barrier, inc=1, device_id=self.other_core(), device_id_type=MESH)
         for i in range(1, 16):
             pl.semaphore_signal(barrier, inc=1, device_id=self.in_plane(i), device_id_type=MESH)
-            pl.semaphore_signal(barrier, inc=1, device_id=self.in_plane(i, 1), device_id_type=MESH)
             pl.semaphore_signal(barrier, inc=1, device_id=self.in_text(i), device_id_type=MESH)
 
     def met(self):
-        pl.semaphore_wait(pltpu.get_barrier_semaphore(), 46)
+        pl.semaphore_wait(pltpu.get_barrier_semaphore(), 31)
 
 
 class Sends:
@@ -99,7 +97,9 @@
     return jnp.where(slot < length, 1.0 / length, 0.0)
 
 
-COPIES = 2 + 3 + 6 + 6 + 3 + 1 + 1 + 15 + 15 + 15 + 1 + 15 + 31 + 15 + 15 + 3 + 12 + 15 + 15 + 7 + 7 + 3 + 12 + 16 + 1
+COPIES = sum(
+    (2, 3, 6, 7, 3, 6, 1, 1, 15, 3, 12, 15, 7, 15, 15, 3, 12, 16, 1, 15, 15, 1, 15, 7, 8, 7, 1)
+)
 SCORE_SCALE = 256 ** (-0.5)
 IMAGES = 512
 
@@ -109,7 +109,7 @@
     up_h, down_h, proj_h, qg_h,
     plen, tok, ngain, w_up, w_down, fgain, w_proj, quer, assign, valid,
     nrm, gd, cs, cr, xs, xr, ys, yr, lo, wfull, frow, psend, prow, allf, vcol, score, sgrad, qg, up_o, down_o, proj_o,
-    fcs, fcr, ts, tr, rsend, rgot, grow, pj, pjf, og, h_all, n_t, ogz, dg, dp, dpr,
+    fcs, fcr, ts, tr, ps, pr, fgb, gs, cols, scg, gz, pj, pjf, oh, og, h_all, n_t, ohz, dg, dp, dpr,
     us, uyr, uz, ur, load_sems, store_sems, send_sems, recv_sems,
 ):
     me = Place()
@@ -166,6 +166,7 @@
     vcol[...] = jnp.broadcast_to(valid[...].astype(F32), (128, 256)).T
     for copy in w_y:
         copy.wait_recv()
+    w_x = [send(wfull.at[:, x, core], wfull.at[:, x, core], me.along_x(i)) for i in (1, 2, 3)]
     to_y = []
     for j in range(2):
         for copy in to_x[j]:
@@ -175,7 +176,9 @@
             total += xr[j, i].astype(F32)
         ys[j] = total.astype(BF16)
         to_y.append([send(ys.at[j, lax.rem(y + i, 4)], yr.at[j, i - 1], me.along_y(i)) for i in (2, 1, 3)])
-    w_x = [send(wfull.at[:, x, core], wfull.at[:, x, core], me.along_x(i)) for i in (1, 2, 3)]
+    for copy in w_x:
+        copy.wait_recv()
+    w_core = send(wfull.at[:, :, core], wfull.at[:, :, core], me.other_core())
     for j in range(2):
         for copy in to_y[j]:
             copy.wait_recv()
@@ -184,9 +187,6 @@
             total += yr[j, i].astype(F32)
         lo[core, :, j * 512 : (j + 1) * 512] = total
     half = send(lo.at[core], lo.at[core], me.other_core())
-    for copy in w_x:
-        copy.wait_recv()
-    w_core = send(wfull.at[:, :, core], wfull.at[:, :, core], me.other_core())
     half.wait_recv()
     layer_out = tok[at(chip, 16), :].astype(F32) + jnp.concatenate([lo[0], lo[1]], axis=1)
     centred = layer_out - jnp.mean(layer_out, axis=1, keepdims=True)
@@ -200,9 +200,24 @@
     feat = dot(jnp.broadcast_to(pooled_low, (16, 2048)), wfull[...].reshape(2048, 256))
     frow[chip] = feat[:1].astype(BF16).astype(F32)
     to_plane = [send(frow.at[chip], frow.at[chip], me.in_plane(i)) for i in range(1, 16)]
+    hat_low = out_hat.astype(BF16)
+    oh[0, chip] = hat_low[:, :1024]
+    oh[1, chip] = hat_low[:, 1024:]
+    own = oh.at[core, chip]
+    oh_y = [send(own, own, me.along_y(i)) for i in (2, 1, 3)]
+    oh_waves = [[send(own, own, me.along_x(i)) for i in (2, 1, 3)]]
+    for k in range(16):
+        ohz[k] = hat_low[:, 128 * k : 128 * k + 128]
+    dg[core, chip, z] = ohz[2 * z + core]
+    z_to = [
+        send(ohz.at[lax.rem(z + i, 8) * 2 + core], dg.at[core, chip, z], me.along_z(i))
+        for i in (4, 3, 5, 2, 6, 1, 7)
+    ]
     rounded = pooled_low.astype(F32)
+    diagonal = lax.broadcasted_iota(jnp.int32, (16, 128), 0) == lax.broadcasted_iota(jnp.int32, (16, 128), 1)
+    scale_row = jnp.sum(jnp.where(diagonal, pool_weight * inv_scale, 0.0), axis=0, keepdims=True)
     for k in range(16):
-        psend[k] = rounded[:, k * 128 : (k + 1) * 128]
+        psend[k] = jnp.concatenate([rounded[:, k * 128 : (k + 1) * 128], scale_row], axis=1)
     prow[chip] = psend[chip]
     pooled_to = [send(psend.at[lax.rem(chip + i, 16)], prow.at[chip], me.in_plane(i)) for i in range(1, 16)]
     n_t[...] = nrm[...].T
@@ -210,9 +225,32 @@
         copy.wait_recv()
     allf[t] = jnp.concatenate([frow[k] for k in range(16)], axis=0).astype(BF16)
     to_text = [send(allf.at[t], allf.at[t], me.in_text(i)) for i in range(1, 16)]
+
+    def spread_y(to_y, buf, waves, to_other):
+        for copy, i in ((to_y[1], 1), (to_y[2], 3), (to_y[0], 2)):
+            copy.wait_recv()
+            block = buf.at[core, lax.rem(y + 4 - i, 4) * 4 + x]
+            waves.append([send(block, block, me.along_x(j)) for j in (2, 1, 3)])
+            to_other.append(send(block, block, me.other_core()))
+
+    def spread_x(buf, waves, to_other):
+        for wave, i in zip(waves, (0, 1, 3, 2)):
+            for copy, j in zip(wave, (2, 1, 3)):
+                copy.wait_recv()
+                block = buf.at[core, lax.rem(y + 4 - i, 4) * 4 + lax.rem(x + 4 - j, 4)]
+                to_other.append(send(block, block, me.other_core()))
+
+    oh_other = []
+    spread_y(oh_y, oh, oh_waves, oh_other)
     for copy in pooled_to:
         copy.wait_recv()
-    pj[t, :, 256:] = jnp.concatenate([prow[k] for k in range(16)], axis=0).astype(BF16)
+    pj[t, :, 256:] = jnp.concatenate([prow[k] for k in range(16)], axis=0)[:, :128].astype(BF16)
+    for copy in z_to:
+        copy.wait_recv()
+    own = dg.at[core, chip]
+    dg_y = [send(own, own, me.along_y(i)) for i in (2, 1, 3)]
+    dg_waves = [[send(own, own, me.along_x(i)) for i in (2, 1, 3)]]
+    dg_other = [send(own, own, me.other_core())]
     for copy in to_text:
         copy.wait_recv()
 
@@ -241,6 +279,7 @@
     mine = jnp.where(core == 0, halves[0], halves[1])
     fcs[...] = jnp.where(core == 0, halves[1], halves[0]).astype(BF16)
     to_core = send(fcs, fcr, me.other_core())
+    spread_y(dg_y, dg, dg_waves, dg_other)
     to_core.wait_recv()
     ts[...] = (mine + fcr[...].astype(F32)).astype(BF16).reshape(16, 16, 128)
     to_text2 = [send(ts.at[lax.rem(t + i, 16)], tr.at[i - 1], me.in_text(i)) for i in range(1, 16)]
@@ -248,86 +287,44 @@
     qg[pl.ds(0, 1100, stride=2), :] = query_grad[:, :128]
     qg[pl.ds(1, 1100, stride=2), :] = query_grad[:, 128:]
     store(qg, qg_h)
+    spread_x(oh, oh_waves, oh_other)
+    for copy in oh_other:
+        copy.wait_recv()
     total = ts[t].astype(F32)
     for i in range(15):
         to_text2[i].wait_recv()
         total += tr[i].astype(F32)
+    ps[...] = total.astype(BF16)
+    to_plane2 = [send(ps, pr.at[i - 1], me.in_plane(i)) for i in range(1, 16)]
+    spread_x(dg, dg_waves, dg_other)
+    for i in range(15):
+        to_plane2[i].wait_recv()
+        total += pr[i].astype(F32)
+    fgb[core] = total
+    half = send(fgb.at[core], fgb.at[core], me.other_core())
+    half.wait_recv()
+    feat_grad = jnp.concatenate([fgb[0], fgb[1]], axis=1)
+    pj[t, :, :256] = feat_grad.astype(BF16)
+    pj_to = [send(pj.at[t], pj.at[t], me.in_text(i)) for i in range(1, 16)]
+    high = feat_grad.astype(BF16)
+    middle = (feat_grad - high.astype(F32)).astype(BF16)
+    low = (feat_grad - high.astype(F32) - middle.astype(F32)).astype(BF16)
+    parts = dot(jnp.concatenate([high, middle, low], axis=0), wfull[...].reshape(2048, 256), ((1,), (1,)))
+    gs[...] = (parts[:16] + parts[16:32] + parts[32:]) * fgain[...]
+    lane = lax.broadcasted_iota(jnp.int32, (16, 128), 1)
     for k in range(16):
-        rsend[k] = total[k : k + 1]
-    rgot[core, chip] = rsend[chip]
-    to_rows = [send(rsend.at[chip], rgot.at[core, chip], me.other_core())]
-    for i in range(1, 16):
-        there = rsend.at[lax.rem(chip + i, 16)]
-        to_rows.append(send(there, rgot.at[core, chip], me.in_plane(i)))
-        to_rows.append(send(there, rgot.at[core, chip], me.in_plane(i, 1)))
-    for copy in to_rows:
-        copy.wait_recv()
-    sums = []
-    for c in range(2):
-        total = rgot[c, 0]
-        for k in range(1, 16):
-            total += rgot[c, k]
-        sums.append(total)
-    row = jnp.concatenate(sums, axis=1)
-    grow[chip] = row
-    high = row.astype(BF16).astype(F32)
-    middle = (row - high).astype(BF16).astype(F32)
-    low = row - high - middle
-    part = lax.broadcasted_iota(jnp.int32, (16, 256), 0)
-    rows = jnp.where(part == 0, high, jnp.where(part == 1, middle, jnp.where(part == 2, low, 0.0)))
-    pooled_grad = jnp.sum(
-        dot(rows.astype(BF16), wfull[...].reshape(2048, 256), ((1,), (1,))), axis=0, keepdims=True
-    )
-    hat = pooled_grad * fgain[...]
-    first = jnp.mean(hat, axis=1, keepdims=True)
-    second = jnp.mean(hat * out_hat, axis=1, keepdims=True)
-    out_grad = ((hat - first - out_hat * second) * (pool_weight * inv_scale)).astype(BF16)
-    og[0, y, x] = out_grad[:, :1024]
-    og[1, y, x] = out_grad[:, 1024:]
-    own = og.at[core, y, x]
-    to_y = [send(own, own, me.along_y(i)) for i in (2, 1, 3)]
-    waves = [[send(own, own, me.along_x(i)) for i in (2, 1, 3)]]
-    for k in range(16):
-        ogz[k] = out_grad[:, 128 * k : 128 * k + 128]
-    dg[core, y, x, z] = ogz[2 * z + core]
-    z_to = [
-        send(ogz.at[lax.rem(z + i, 8) * 2 + core], dg.at[core, y, x, z], me.along_z(i))
-        for i in (4, 3, 5, 2, 6, 1, 7)
-    ]
-    to_grow = [send(grow.at[chip], grow.at[chip], me.in_plane(i)) for i in range(1, 16)]
-
-    def spread_y(to_y, buf, waves, to_other):
-        for copy, i in ((to_y[1], 1), (to_y[2], 3), (to_y[0], 2)):
-            copy.wait_recv()
-            block = buf.at[core, lax.rem(y + 4 - i, 4), x]
-            waves.append([send(block, block, me.along_x(j)) for j in (2, 1, 3)])
-            to_other.append(send(block, block, me.other_core()))
-
-    def spread_x(buf, waves, to_other):
-        for wave, i in zip(waves, (0, 1, 3, 2)):
-            for copy, j in zip(wave, (2, 1, 3)):
-                copy.wait_recv()
-                block = buf.at[core, lax.rem(y + 4 - i, 4), lax.rem(x + 4 - j, 4)]
-                to_other.append(send(block, block, me.other_core()))
-
-    to_other = []
-    spread_y(to_y, og, waves, to_other)
-    for copy in z_to:
-        copy.wait_recv()
-    own = dg.at[core, y, x]
-    dg_y = [send(own, own, me.along_y(i)) for i in (2, 1, 3)]
-    dg_waves = [[send(own, own, me.along_x(i)) for i in (2, 1, 3)]]
-    dg_other = [send(own, own, me.other_core())]
-    for copy in to_grow:
-        copy.wait_recv()
-    pj[t, :, :256] = jnp.concatenate([grow[k] for k in range(16)], axis=0).astype(BF16)
-    pj_to = [send(pj.at[t], pj.at[t], me.in_text(i)) for i in range(1, 16)]
-    spread_x(og, waves, to_other)
-    spread_y(dg_y, dg, dg_waves, dg_other)
-    for copy in to_other:
-        copy.wait_recv()
-    halves = [og[h].reshape(256, 1024) for h in range(2)]
-    hidden_grad = dot(halves[0], w_down[:, :1024], ((1,), (1,))) + dot(halves[1], w_down[:, 1024:], ((1,), (1,)))
+        hat = gs[k : k + 1, :]
+        out_hat = jnp.concatenate([oh[0, k], oh[1, k]], axis=1).astype(F32)
+        first = jnp.mean(hat, axis=1, keepdims=True)
+        second = jnp.mean(hat * out_hat, axis=1, keepdims=True)
+        scale = jnp.sum(jnp.where(diagonal, prow[k][:, 128:], 0.0), axis=1, keepdims=True)
+        og[16 * k : 16 * k + 16, :] = ((hat - first - out_hat * second) * scale).astype(BF16)
+        cols[16 * k : 16 * k + 16, :] = jnp.where(
+            lane == 0, scale, jnp.where(lane == 1, first, jnp.where(lane == 2, second, 0.0))
+        )
+    scg[z] = cols[...].T[:8]
+    sc_to = [send(scg.at[z], scg.at[z], me.along_z(i)) for i in (4, 3, 5, 2, 6, 1, 7)]
+    hidden_grad = dot(og[...], w_down[...], ((1,), (1,)))
     pre_grad = (hidden_grad * gd[...]).astype(BF16)
     us[...] = dot(n_t[...], pre_grad).astype(BF16).reshape(8, 2, 128, 256)
     order = (4, 3, 5, 2, 6, 1, 7, 0)
@@ -342,24 +339,26 @@
 
     for i in order[:4]:
         onward(i)
-    spread_x(dg, dg_waves, dg_other)
+    for copy in dg_other + h_to + sc_to + pj_to:
+        copy.wait_recv()
+    fg_group = jnp.concatenate([pj[2 * k + yl, :, :256] for k in range(8)], axis=0)
+    w_group = wfull[z // 2, pl.ds(2 * lax.rem(z, 2), 2)].reshape(256, 256)
+    gz[...] = dot(fg_group, w_group, ((1,), (1,))) * fgain[:, at(z, 256)]
+    product = jnp.zeros((256, 256), F32)
+    for k in range(8):
+        turned = jnp.concatenate([scg[k], jnp.zeros((120, 256), F32)], axis=0).T
+        scale, first, second = turned[:, :1], turned[:, 1:2], turned[:, 2:3]
+        hat = jnp.broadcast_to(gz[16 * k : 16 * k + 16][:, None, :], (16, 16, 256)).reshape(256, 256)
+        out_hat = jnp.concatenate([dg[h, :, k].reshape(256, 128) for h in range(2)], axis=1).astype(F32)
+        grads = ((hat - first - out_hat * second) * scale).astype(BF16)
+        product += dot(h_all[k], grads)
+    lower, upper = product[:, :128], product[:, 128:]
+    dp[...] = jnp.where(yl == 0, upper, lower).astype(BF16)
+    down_own = jnp.where(yl == 0, lower, upper)
+    dp_to = send(dp, dpr, me.across())
     for i in order[4:6]:
         onward(i)
-    for copy in dg_other + h_to:
-        copy.wait_recv()
-
-    def down_product(h):
-        total = dot(h_all[0], dg[h, :, :, 0].reshape(256, 128))
-        for k in range(1, 8):
-            total += dot(h_all[k], dg[h, :, :, k].reshape(256, 128))
-        return total
-
-    dp[...] = down_product(1 - yl).astype(BF16)
-    dp_to = send(dp, dpr, me.across())
     onward(order[6])
-    down_own = down_product(yl)
-    for copy in pj_to:
-        copy.wait_recv()
     pjf[...] = dot(pj[:, :, 256:].reshape(256, 128), pj[:, :, :256].reshape(256, 256), ((0,), (0,)))
     proj_o[...] = pjf[at(core, 64), :]
     store(proj_o, proj_h)
@@ -441,8 +440,8 @@
             pltpu.VMEM((2, 16, 1024), F32),
             pltpu.VMEM((4, 4, 2, 64, 256), BF16),
             pltpu.VMEM((16, 1, 256), F32),
-            pltpu.VMEM((16, 1, 128), F32),
-            pltpu.VMEM((16, 1, 128), F32),
+            pltpu.VMEM((16, 1, 256), F32),
+            pltpu.VMEM((16, 1, 256), F32),
             pltpu.VMEM((16, 16, 256), BF16),
             pltpu.VMEM((256, 128), F32),
             pltpu.VMEM((256, 1100), F32),
@@ -455,16 +454,21 @@
             pltpu.VMEM((256, 128), BF16),
             pltpu.VMEM((16, 16, 128), BF16),
             pltpu.VMEM((15, 16, 128), BF16),
-            pltpu.VMEM((16, 1, 128), F32),
-            pltpu.VMEM((2, 16, 1, 128), F32),
-            pltpu.VMEM((16, 1, 256), F32),
+            pltpu.VMEM((16, 128), BF16),
+            pltpu.VMEM((15, 16, 128), BF16),
+            pltpu.VMEM((2, 16, 128), F32),
+            pltpu.VMEM((16, 2048), F32),
+            pltpu.VMEM((256, 128), F32),
+            pltpu.VMEM((8, 8, 256), F32),
+            pltpu.VMEM((128, 256), F32),
             pltpu.VMEM((16, 16, 384), BF16),
             pltpu.VMEM((128, 256), F32),
-            pltpu.VMEM((2, 4, 4, 16, 1024), BF16),
+            pltpu.VMEM((2, 16, 16, 1024), BF16),
+            pltpu.VMEM((256, 2048), BF16),
             pltpu.VMEM((8, 256, 256), BF16),
             pltpu.VMEM((2048, 256), BF16),
             pltpu.VMEM((16, 16, 128), BF16),
-            pltpu.VMEM((2, 4, 4, 8, 16, 128), BF16),
+            pltpu.VMEM((2, 16, 8, 16, 128), BF16),
             pltpu.VMEM((256, 128), BF16),
             pltpu.VMEM((256, 128), BF16),
             pltpu.VMEM((8, 2, 128, 256), BF16),

time: 102 us -> 91.8 us (0.900)
  Pallas kernels: 101 us -> 91 us
    pallas_call x1, Pallas kernels: 98.9 us -> 88.8 us  [step(): pl.pallas_call(step_kernel, name='step', in_specs=[pl.BlockSpec(memory_sp...]
where the time goes in v4:
time: 91.8 us; the launch traced here: 91.6 us
  Pallas kernels  91 us (99%)
    pallas_call x1, Pallas kernels, step(): pl.pallas_call(step_kernel, name='step', in_specs=[pl.BlockSpec(memory_sp...  88.8 us
    pallas_call x1, Pallas kernels, hand_out(): pl.pallas_call(hand_out_kernel, name='hand_out', in_specs=[pl.BlockSpec(m...  2.17 us

profile of v4, /device:TPU:1, one launch (start us, length us, event | category | flops | bytes accessed | tf_op | source)
XLA Modules:
  0.0 91.6 jit_solution(7410508453300120040)
XLA Ops:
  0.6 88.8 %step.1 = (f32[128,256]{1,0:T(8,128)}, f32[256,128]{1,0:T(8,128)}, f32[64,256]{1,0:T(8,128)}, f32[2200,128]{1,0:T(8,128)}) custom-call(s32[1,16]{1,0:T(1,128)} %bitcast.10, bf16[256,2048]{1,0:T(8,128)(2,1)} %bitcast.6, f32[1,2048]{1,0:T(1,128)} %bitcast.8, bf16[2048,256]{1,0:T(8,128)(2,1)} %w_up_h.1, bf16[256,2048]{1,0:T(8,128)(2,1)} %w_down_h.1, ...), custom_call_target="tpu_custom_call" | custom-call | tf_op jit(solution)/shard_map/step/pallas_call | solution.py:410
  89.4 2.2 %hand_out.1 = (f32[128,256]{1,0:T(8,128)}, f32[256,128]{1,0:T(8,128)}, f32[64,256]{1,0:T(8,128)}, f32[2200,128]{1,0:T(8,128)}) custom-call(f32[128,256]{1,0:T(8,128)} %get-tuple-element.12.a, f32[256,128]{1,0:T(8,128)} %get-tuple-element.13.b, f32[64,256]{1,0:T(8,128)} %get-tuple-element.14.c, f32[2200,128]{1,0:T(8,128)} %get-tuple-element.15.d), custom_call_target="tpu_custom_call" | custom-call | tf_op jit(solution)/shard_map/hand_out/pallas_call | solution.py:398

commit v5 on v4

--- a/solution.py
+++ b/solution.py
@@ -98,7 +98,7 @@
 
 
 COPIES = sum(
-    (2, 3, 6, 7, 3, 6, 1, 1, 15, 3, 12, 15, 7, 15, 15, 3, 12, 16, 1, 15, 15, 1, 15, 7, 8, 7, 1)
+    (2, 3, 6, 7, 3, 6, 1, 1, 15, 3, 12, 15, 7, 15, 15, 3, 12, 16, 1, 15, 15, 1, 15, 7, 8, 8, 1)
 )
 SCORE_SCALE = 256 ** (-0.5)
 IMAGES = 512
@@ -115,7 +115,6 @@
     me = Place()
     send = Sends(send_sems, recv_sems)
     core, chip, x, y, t, z, yl = me.core, me.chip, me.x, me.y, me.t, me.z, me.yl
-    me.greet()
     loads = {}
     for n, (name, src, dst) in enumerate((
         ("tok", tok_h, tok), ("ngain", ngain_h, ngain), ("w_up", w_up_h, w_up), ("w_down", w_down_h, w_down),
@@ -124,6 +123,7 @@
     )):
         loads[name] = pltpu.make_async_copy(src, dst, load_sems.at[n])
         loads[name].start()
+    me.greet()
     stores = []
 
     def store(src, dst):
@@ -251,29 +251,35 @@
     dg_y = [send(own, own, me.along_y(i)) for i in (2, 1, 3)]
     dg_waves = [[send(own, own, me.along_x(i)) for i in (2, 1, 3)]]
     dg_other = [send(own, own, me.other_core())]
-    for copy in to_text:
-        copy.wait_recv()
-
-    features = allf[...].reshape(256, 256)
-    score[...] = dot(features, quer[...], ((1,), (1,)))
     chosen = assign[...]
 
-    @pl.loop(0, 16)
-    def _(r):
-        spot = at(r, 16)
-        s = score[spot, :] * SCORE_SCALE + LOGIT_BIAS
-        concept = lax.broadcasted_iota(jnp.int32, (16, 1100), 0) + r * 16
-        hit = concept == chosen
-        u = jnp.where(hit, -s, s)
-        e = jnp.exp(-jnp.abs(u))
-        more = 1.0 / (1.0 + e)
-        less = e * more
-        p = jnp.where(u >= 0.0, more, less)
-        q = jnp.where(u >= 0.0, less, more)
-        soft = jnp.maximum(u, 0.0) + jnp.log1p(e)
-        factor = jnp.where(hit, -ALPHA, 1.0 - ALPHA) * vcol[spot, :1]
-        sgrad[spot, :] = (factor * p * p * (p + 2.0 * q * soft)).astype(BF16)
-
+    def query_half(half, start):
+        blocks = [lax.rem(t + start + n, 16) for n in range(8)]
+        for n in range(8):
+            back = (16 - start - n) % 16
+            if back:
+                to_text[back - 1].wait_recv()
+        score[half] = dot(jnp.concatenate([allf[b] for b in blocks], axis=0), quer[...], ((1,), (1,)))
+
+        @pl.loop(0, 8)
+        def _(n):
+            block = lax.rem(t + start + n, 16)
+            spot = at(block, 16)
+            s = score[half, at(n, 16), :] * SCORE_SCALE + LOGIT_BIAS
+            concept = lax.broadcasted_iota(jnp.int32, (16, 1100), 0) + block * 16
+            hit = concept == chosen
+            u = jnp.where(hit, -s, s)
+            e = jnp.exp(-jnp.abs(u))
+            more = 1.0 / (1.0 + e)
+            less = e * more
+            p = jnp.where(u >= 0.0, more, less)
+            q = jnp.where(u >= 0.0, less, more)
+            soft = jnp.maximum(u, 0.0) + jnp.log1p(e)
+            factor = jnp.where(hit, -ALPHA, 1.0 - ALPHA) * vcol[spot, :1]
+            sgrad[spot, :] = (factor * p * p * (p + 2.0 * q * soft)).astype(BF16)
+
+    query_half(0, 13)
+    query_half(1, 5)
     terms = dot(sgrad[...], quer[...]) * (SCORE_SCALE / IMAGES)
     halves = (terms[:, :128], terms[:, 128:])
     mine = jnp.where(core == 0, halves[0], halves[1])
@@ -283,7 +289,7 @@
     to_core.wait_recv()
     ts[...] = (mine + fcr[...].astype(F32)).astype(BF16).reshape(16, 16, 128)
     to_text2 = [send(ts.at[lax.rem(t + i, 16)], tr.at[i - 1], me.in_text(i)) for i in range(1, 16)]
-    query_grad = dot(sgrad[...], features, ((0,), (0,))) * SCORE_SCALE
+    query_grad = dot(sgrad[...], allf[...].reshape(256, 256), ((0,), (0,))) * SCORE_SCALE
     qg[pl.ds(0, 1100, stride=2), :] = query_grad[:, :128]
     qg[pl.ds(1, 1100, stride=2), :] = query_grad[:, 128:]
     store(qg, qg_h)
@@ -328,17 +334,23 @@
     pre_grad = (hidden_grad * gd[...]).astype(BF16)
     us[...] = dot(n_t[...], pre_grad).astype(BF16).reshape(8, 2, 128, 256)
     order = (4, 3, 5, 2, 6, 1, 7, 0)
-    up_y, up_z = {}, {}
+    up_y = {}
     for i in order:
         up_y[i] = send(us.at[lax.rem(z + i, 8), 1 - yl], uyr.at[i], me.across())
 
-    def onward(i):
+    def pair_sum(i):
         up_y[i].wait_recv()
-        uz[i - 1] = (us[lax.rem(z + i, 8), yl].astype(F32) + uyr[i].astype(F32)).astype(BF16)
-        up_z[i] = send(uz.at[i - 1], ur.at[i - 1], me.along_z(i))
-
-    for i in order[:4]:
-        onward(i)
+        return us[lax.rem(z + i, 8), yl].astype(F32) + uyr[i].astype(F32)
+
+    near, far = pl.ds(0, 64), pl.ds(64, 64)
+    uz[3] = pair_sum(4).astype(BF16)
+    relay = {
+        2: send(uz.at[3, near], ur.at[4, near], me.along_z(2)),
+        6: send(uz.at[3, far], ur.at[4, far], me.along_z(6)),
+    }
+    for i, via, to in ((3, 2, 1), (5, 6, 7)):
+        uz[i - 1] = pair_sum(i).astype(BF16)
+        relay[to] = send(uz.at[i - 1], ur.at[5 if i == 3 else 6], me.along_z(via))
     for copy in dg_other + h_to + sc_to + pj_to:
         copy.wait_recv()
     fg_group = jnp.concatenate([pj[2 * k + yl, :, :256] for k in range(8)], axis=0)
@@ -356,20 +368,29 @@
     dp[...] = jnp.where(yl == 0, upper, lower).astype(BF16)
     down_own = jnp.where(yl == 0, lower, upper)
     dp_to = send(dp, dpr, me.across())
-    for i in order[4:6]:
-        onward(i)
-    onward(order[6])
+    last = {}
+    for i in (2, 6, 1, 7):
+        total = pair_sum(i)
+        relay[i].wait_recv()
+        if i == 2:
+            uz[1, near] = (total[:64] + ur[4, near].astype(F32)).astype(BF16)
+            uz[1, far] = total[64:].astype(BF16)
+        elif i == 6:
+            uz[5, near] = total[:64].astype(BF16)
+            uz[5, far] = (total[64:] + ur[4, far].astype(F32)).astype(BF16)
+        else:
+            uz[i - 1] = (total + ur[5 if i == 1 else 6].astype(F32)).astype(BF16)
+        last[i] = send(uz.at[i - 1], ur.at[(2, 6, 1, 7).index(i)], me.along_z(i))
     pjf[...] = dot(pj[:, :, 256:].reshape(256, 128), pj[:, :, :256].reshape(256, 256), ((0,), (0,)))
     proj_o[...] = pjf[at(core, 64), :]
     store(proj_o, proj_h)
     dp_to.wait_recv()
     down_o[...] = down_own + dpr[...].astype(F32)
     store(down_o, down_h)
-    up_y[0].wait_recv()
-    total = us[z, yl].astype(F32) + uyr[0].astype(F32)
-    for i in (4, 3, 5, 2, 6, 1, 7):
-        up_z[i].wait_recv()
-        total += ur[i - 1].astype(F32)
+    total = pair_sum(0)
+    for n, i in enumerate((2, 6, 1, 7)):
+        last[i].wait_recv()
+        total += ur[n].astype(F32)
     up_o[...] = total
     store(up_o, up_h)
     send.drain()
@@ -444,7 +465,7 @@
             pltpu.VMEM((16, 1, 256), F32),
             pltpu.VMEM((16, 16, 256), BF16),
             pltpu.VMEM((256, 128), F32),
-            pltpu.VMEM((256, 1100), F32),
+            pltpu.VMEM((2, 128, 1100), F32),
             pltpu.VMEM((256, 1100), BF16),
             pltpu.VMEM((2200, 128), F32),
             pltpu.VMEM((128, 256), F32),

time: 91.8 us -> 88.5 us (0.964)
  Pallas kernels: 91 us -> 87.7 us
    pallas_call x1, Pallas kernels: 88.8 us -> 85.6 us  [step(): pl.pallas_call(step_kernel, name='step', in_specs=[pl.BlockSpec(memory_sp...]
where the time goes in v5:
time: 88.5 us; the launch traced here: 88.4 us
  Pallas kernels  87.7 us (99%)
    pallas_call x1, Pallas kernels, step(): pl.pallas_call(step_kernel, name='step', in_specs=[pl.BlockSpec(memory_sp...  85.6 us
    pallas_call x1, Pallas kernels, hand_out(): pl.pallas_call(hand_out_kernel, name='hand_out', in_specs=[pl.BlockSpec(m...  2.17 us

profile of v5, /device:TPU:1, one launch (start us, length us, event | category | flops | bytes accessed | tf_op | source)
XLA Modules:
  0.0 88.4 jit_solution(7386345397318661347)
XLA Ops:
  0.6 85.6 %step.1 = (f32[128,256]{1,0:T(8,128)}, f32[256,128]{1,0:T(8,128)}, f32[64,256]{1,0:T(8,128)}, f32[2200,128]{1,0:T(8,128)}) custom-call(s32[1,16]{1,0:T(1,128)} %bitcast.10, bf16[256,2048]{1,0:T(8,128)(2,1)} %bitcast.6, f32[1,2048]{1,0:T(1,128)} %bitcast.8, bf16[2048,256]{1,0:T(8,128)(2,1)} %w_up_h.1, bf16[256,2048]{1,0:T(8,128)(2,1)} %w_down_h.1, ...), custom_call_target="tpu_custom_call" | custom-call | tf_op jit(solution)/shard_map/step/pallas_call | solution.py:431
  86.2 2.2 %hand_out.1 = (f32[128,256]{1,0:T(8,128)}, f32[256,128]{1,0:T(8,128)}, f32[64,256]{1,0:T(8,128)}, f32[2200,128]{1,0:T(8,128)}) custom-call(f32[128,256]{1,0:T(8,128)} %get-tuple-element.12.a, f32[256,128]{1,0:T(8,128)} %get-tuple-element.13.b, f32[64,256]{1,0:T(8,128)} %get-tuple-element.14.c, f32[2200,128]{1,0:T(8,128)} %get-tuple-element.15.d), custom_call_target="tpu_custom_call" | custom-call | tf_op jit(solution)/shard_map/hand_out/pallas_call | solution.py:419

commit v6 on v5

--- a/solution.py
+++ b/solution.py
@@ -160,7 +160,7 @@
         to_x.append(
             [send(xs.at[j, :, lax.rem(x + i, 4)], xr.at[j, i - 1], me.along_x(i)) for i in (2, 1, 3)]
         )
-    h_to = [send(h_all.at[z], h_all.at[z], me.along_z(i)) for i in (4, 3, 5, 2, 6, 1, 7)]
+    h_to = [send(h_all.at[z], h_all.at[z], me.along_z(i)) for i in (4, 3, 5)]
     for name in ("plen", "fgain", "quer", "assign", "valid"):
         loads[name].wait()
     vcol[...] = jnp.broadcast_to(valid[...].astype(F32), (128, 256)).T
@@ -242,15 +242,6 @@
 
     oh_other = []
     spread_y(oh_y, oh, oh_waves, oh_other)
-    for copy in pooled_to:
-        copy.wait_recv()
-    pj[t, :, 256:] = jnp.concatenate([prow[k] for k in range(16)], axis=0)[:, :128].astype(BF16)
-    for copy in z_to:
-        copy.wait_recv()
-    own = dg.at[core, chip]
-    dg_y = [send(own, own, me.along_y(i)) for i in (2, 1, 3)]
-    dg_waves = [[send(own, own, me.along_x(i)) for i in (2, 1, 3)]]
-    dg_other = [send(own, own, me.other_core())]
     chosen = assign[...]
 
     def query_half(half, start):
@@ -285,10 +276,19 @@
     mine = jnp.where(core == 0, halves[0], halves[1])
     fcs[...] = jnp.where(core == 0, halves[1], halves[0]).astype(BF16)
     to_core = send(fcs, fcr, me.other_core())
-    spread_y(dg_y, dg, dg_waves, dg_other)
     to_core.wait_recv()
     ts[...] = (mine + fcr[...].astype(F32)).astype(BF16).reshape(16, 16, 128)
     to_text2 = [send(ts.at[lax.rem(t + i, 16)], tr.at[i - 1], me.in_text(i)) for i in range(1, 16)]
+    h_to += [send(h_all.at[z], h_all.at[z], me.along_z(i)) for i in (2, 6, 1, 7)]
+    for copy in pooled_to:
+        copy.wait_recv()
+    pj[t, :, 256:] = jnp.concatenate([prow[k] for k in range(16)], axis=0)[:, :128].astype(BF16)
+    for copy in z_to:
+        copy.wait_recv()
+    own = dg.at[core, chip]
+    dg_y = [send(own, own, me.along_y(i)) for i in (2, 1, 3)]
+    dg_waves = [[send(own, own, me.along_x(i)) for i in (2, 1, 3)]]
+    dg_other = [send(own, own, me.other_core())]
     query_grad = dot(sgrad[...], allf[...].reshape(256, 256), ((0,), (0,))) * SCORE_SCALE
     qg[pl.ds(0, 1100, stride=2), :] = query_grad[:, :128]
     qg[pl.ds(1, 1100, stride=2), :] = query_grad[:, 128:]
@@ -302,7 +302,7 @@
         total += tr[i].astype(F32)
     ps[...] = total.astype(BF16)
     to_plane2 = [send(ps, pr.at[i - 1], me.in_plane(i)) for i in range(1, 16)]
-    spread_x(dg, dg_waves, dg_other)
+    spread_y(dg_y, dg, dg_waves, dg_other)
     for i in range(15):
         to_plane2[i].wait_recv()
         total += pr[i].astype(F32)
@@ -337,6 +337,8 @@
     up_y = {}
     for i in order:
         up_y[i] = send(us.at[lax.rem(z + i, 8), 1 - yl], uyr.at[i], me.across())
+
+    spread_x(dg, dg_waves, dg_other)
 
     def pair_sum(i):
         up_y[i].wait_recv()

time: 88.5 us -> 86.1 us (0.973)
  Pallas kernels: 87.7 us -> 85.3 us
    pallas_call x1, Pallas kernels: 85.6 us -> 83.1 us  [step(): pl.pallas_call(step_kernel, name='step', in_specs=[pl.BlockSpec(memory_sp...]
where the time goes in v6:
time: 86.1 us; the launch traced here: 85.9 us
  Pallas kernels  85.3 us (99%)
    pallas_call x1, Pallas kernels, step(): pl.pallas_call(step_kernel, name='step', in_specs=[pl.BlockSpec(memory_sp...  83.1 us
    pallas_call x1, Pallas kernels, hand_out(): pl.pallas_call(hand_out_kernel, name='hand_out', in_specs=[pl.BlockSpec(m...  2.17 us

profile of v6, /device:TPU:1, one launch (start us, length us, event | category | flops | bytes accessed | tf_op | source)
XLA Modules:
  0.0 85.9 jit_solution(15019330320107214430)
XLA Ops:
  0.6 83.1 %step.1 = (f32[128,256]{1,0:T(8,128)}, f32[256,128]{1,0:T(8,128)}, f32[64,256]{1,0:T(8,128)}, f32[2200,128]{1,0:T(8,128)}) custom-call(s32[1,16]{1,0:T(1,128)} %bitcast.10, bf16[256,2048]{1,0:T(8,128)(2,1)} %bitcast.6, f32[1,2048]{1,0:T(1,128)} %bitcast.8, bf16[2048,256]{1,0:T(8,128)(2,1)} %w_up_h.1, bf16[256,2048]{1,0:T(8,128)(2,1)} %w_down_h.1, ...), custom_call_target="tpu_custom_call" | custom-call | tf_op jit(solution)/shard_map/step/pallas_call | solution.py:433
  83.7 2.2 %hand_out.1 = (f32[128,256]{1,0:T(8,128)}, f32[256,128]{1,0:T(8,128)}, f32[64,256]{1,0:T(8,128)}, f32[2200,128]{1,0:T(8,128)}) custom-call(f32[128,256]{1,0:T(8,128)} %get-tuple-element.12.a, f32[256,128]{1,0:T(8,128)} %get-tuple-element.13.b, f32[64,256]{1,0:T(8,128)} %get-tuple-element.14.c, f32[2200,128]{1,0:T(8,128)} %get-tuple-element.15.d), custom_call_target="tpu_custom_call" | custom-call | tf_op jit(solution)/shard_map/hand_out/pallas_call | solution.py:421
